TPU v7x, 32 devices: a whole 2x2x4 slice. The times are simulated.
32 devices in a mesh: band: 8 (over z, y), dir: 4 (over x, core).
Axes of the slice: x: 2, y: 2, z: 4, core: 2. Of those that a mesh axis runs over, the one named last changes fastest.
Arguments:
- visibilities: float32 [8, 2, 2, 2, 16, 512], P('band'), may hold values from -6 to 6
- coherencies: float32 [8, 16, 2, 2, 2, 16, 512], P('band', 'dir'), may hold values from -1.2 to 1.2
- jones_start: float32 [8, 16, 2, 2, 2, 1024], P('band', 'dir'), may hold values from -3.6 to 3.6
- dual_start: float32 [8, 16, 2, 2, 2, 1024], P('band', 'dir'), may hold values from -6 to 6
- consensus_start: float32 [8, 16, 2, 2, 2, 1024], P(None, 'dir'), may hold values from -1.8 to 1.8
- freq_basis: float32 [8, 8], P('band'), may hold values from -1 to 1
- baseline_station_pairs: int32 [2, 512], replicated, may hold values from 0 to 1023
Outputs:
- jones_final: float32 [8, 16, 2, 2, 2, 1024], P('band', 'dir')
- dual_final: float32 [8, 16, 2, 2, 2, 1024], P('band', 'dir')
- consensus_coeffs: float32 [8, 16, 2, 2, 2, 1024], P(None, 'dir')
All inputs are finite; a program needn't handle non-finite values.
Results may differ from a plain program's by a relative error of at most 0.0003.
Values sent between devices are 32-bit elements; how exact they have to be, the bound alone decides.
A program may use at most 128 MiB of HBM per device.

v0:
```python
import functools

import jax
import jax.numpy as jnp
from jax import lax
from jax.experimental import pallas as pl
from jax.experimental.pallas import tpu as pltpu
from jax.sharding import PartitionSpec as P

ITERS = 3
RHO = 5.0
RIDGE = 0.25
LANES = 128
SUB = 8
PIECES = 3
MESH = pl.DeviceIdType.MESH


def cmul(a, b):
    return (a[0] * b[0] - a[1] * b[1], a[0] * b[1] + a[1] * b[0])


def cmul_conj(a, b):
    return (a[0] * b[0] + a[1] * b[1], a[1] * b[0] - a[0] * b[1])


def cadd(a, b):
    return (a[0] + b[0], a[1] + b[1])


def conj(a):
    return (a[0], -a[1])


def re_mul(a, b):
    return a[0] * b[0] - a[1] * b[1]


def scale(r, a):
    return (r * a[0], r * a[1])


def split_store(ref, rows, value):
    left = value
    for piece in range(PIECES):
        part = left.astype(jnp.bfloat16)
        ref[piece * rows : (piece + 1) * rows, :] = part
        if piece + 1 < PIECES:
            left = left - part.astype(jnp.float32)


def join(value, rows):
    total = value[0:rows]
    for piece in range(1, PIECES):
        total = total + value[piece * rows : (piece + 1) * rows]
    return total


def kernel(
    n_band, n_dir, dirs, times, base, stations,
    vis_far, coh_far, jones0, dual0, coeffs0_far, basis, pairs_ref,
    jones_out, dual_out, coeffs,
    vis, coh, coeffs0, jones, dual, row, ids_col,
    cons, xall, rows_all, weights, gweights,
    gather_hot, scatter_hot, lhs, lhs_n, ends, grams, cross, vals, vals_n, seg, seg_n,
    model, got_a, sum_a, got_b, sum_b, got_c, res,
    load_sem, row_send, row_recv, x_send, x_recv, d_send, d_recv,
):
    f32 = jnp.float32
    nrow = 8 * dirs
    per = stations // LANES
    me = lax.axis_index("band")
    mine = lax.axis_index("dir")
    blocks = base // LANES
    halves = times // SUB
    stages = n_dir.bit_length() - 1

    def at(pos):
        half = pos // (n_band // 2)
        return (1 - half) * (2 * pos) + half * (2 * (n_band - 1 - pos) + 1)

    odd = lax.rem(me, 2)
    pos = (1 - odd) * (me // 2) + odd * (n_band - 1 - me // 2)
    nexts = (at(lax.rem(pos + 1, n_band)), at(lax.rem(pos + n_band - 1, n_band)))

    def flip(stage):
        bit = lax.rem(mine // (1 << stage), 2)
        return mine + (1 - 2 * bit) * (1 << stage)

    own = lax.rem(mine, 2)

    loads = []
    for n, (far, near) in enumerate(((coh_far, coh), (vis_far, vis), (coeffs0_far, coeffs0))):
        loads.append(pltpu.make_async_copy(far, near, load_sem.at[n]))
        loads[-1].start()

    barrier = pltpu.get_barrier_semaphore()
    for step in range(1, n_band):
        pl.semaphore_signal(
            barrier, inc=1, device_id={"band": lax.rem(me + step, n_band)}, device_id_type=MESH
        )
    for stage in range(stages):
        pl.semaphore_signal(barrier, inc=1, device_id={"dir": flip(stage)}, device_id_type=MESH)

    def halves_of(k, v):
        return (k, v // 2, pl.ds(v % 2, per, stride=2), slice(None))

    def packed(k, v):
        return pl.ds((v * dirs + k) * per, per)

    row[...] = jnp.zeros((SUB, LANES), f32)
    for m in range(SUB):
        row[m : m + 1, :] = jnp.full((1, LANES), basis[0, m], f32)
    for k in range(dirs):
        for v in range(8):
            jones[packed(k, v), :] = jones0[halves_of(k, v)]
            dual[packed(k, v), :] = dual0[halves_of(k, v)]

    for j in range(2 * base // LANES):
        lane = (j * LANES) % base
        which = (j * LANES) // base
        ids = jnp.broadcast_to(pairs_ref[which : which + 1, lane : lane + LANES], (LANES, LANES))
        ids_col[j * LANES : (j + 1) * LANES, :] = jnp.transpose(ids)
    step_rows = 32

    def hot_body(i, carry):
        start = pl.multiple_of(i * step_rows, step_rows)
        for j in range(2 * base // LANES):
            lane = slice(j * LANES, (j + 1) * LANES)
            sid = lax.broadcasted_iota(jnp.int32, (step_rows, LANES), 0) + i * step_rows
            which, low = (j * LANES) // base, (j * LANES) % base
            ids = pairs_ref[which : which + 1, low : low + LANES]
            same = sid == jnp.broadcast_to(ids, (step_rows, LANES))
            gather_hot[pl.ds(start, step_rows), lane] = jnp.where(same, 1.0, 0.0).astype(jnp.bfloat16)
        return carry

    lax.fori_loop(0, stations // step_rows, hot_body, 0)

    def hot_body2(i, carry):
        start = pl.multiple_of(i * step_rows, step_rows)
        col = ids_col[pl.ds(start, step_rows), :]
        for j in range(stations // LANES):
            lane = slice(j * LANES, (j + 1) * LANES)
            sid = lax.broadcasted_iota(jnp.int32, (step_rows, LANES), 1) + j * LANES
            scatter_hot[pl.ds(start, step_rows), lane] = jnp.where(sid == col, 1.0, 0.0).astype(jnp.bfloat16)
        return carry

    lax.fori_loop(0, 2 * base // step_rows, hot_body2, 0)

    pl.semaphore_wait(barrier, n_band - 1 + stages)

    row_copies = []
    for step in range(1, n_band):
        copy = pltpu.make_async_remote_copy(
            src_ref=row,
            dst_ref=rows_all.at[step],
            send_sem=row_send.at[step],
            recv_sem=row_recv.at[step],
            device_id={"band": lax.rem(me + step, n_band)},
            device_id_type=MESH,
        )
        copy.start()
        row_copies.append(copy)

    loads[0].wait()

    pairs = [(a, b) for a in range(4) for b in range(a, 4)]

    def gram_body(j, carry):
        lane = pl.ds(pl.multiple_of(j * LANES, LANES), LANES)
        for k in range(dirs):
            c = [
                [coh[k, v, h * SUB : (h + 1) * SUB, lane] for h in range(halves)]
                for v in range(8)
            ]
            for n, (a, b) in enumerate(pairs):
                real = sum(c[a][h] * c[b][h] + c[4 + a][h] * c[4 + b][h] for h in range(halves))
                grams[(2 * n) * dirs + k : (2 * n) * dirs + k + 1, lane] = jnp.sum(real, axis=0, keepdims=True)
                if a != b:
                    imag = sum(c[4 + a][h] * c[b][h] - c[a][h] * c[4 + b][h] for h in range(halves))
                    grams[(2 * n + 1) * dirs + k : (2 * n + 1) * dirs + k + 1, lane] = jnp.sum(
                        imag, axis=0, keepdims=True
                    )
        return carry

    lax.fori_loop(0, blocks, gram_body, 0)

    def gram(a, b):
        if a > b:
            return conj(gram(b, a))
        n = pairs.index((a, b))
        real = grams[(2 * n) * dirs : (2 * n + 1) * dirs, :]
        if a == b:
            return real
        return (real, grams[(2 * n + 1) * dirs : (2 * n + 2) * dirs, :])

    def start_consensus():
        loads[1].wait()
        loads[2].wait()
        for k in range(dirs):
            for v in range(8):
                total = basis[0, 0] * coeffs0[(0,) + halves_of(k, v)]
                for m in range(1, SUB):
                    total = total + basis[0, m] * coeffs0[(m,) + halves_of(k, v)]
                cons[packed(k, v), :] = total

    def solve_weights():
        for copy in row_copies:
            copy.wait()
        rows_all[0] = row[...]
        held = [rows_all[s] for s in range(n_band)]
        columns = []
        for m in range(SUB):
            total = held[0] * held[0][m : m + 1, :]
            for s in range(1, n_band):
                total = total + held[s] * held[s][m : m + 1, :]
            ident = jnp.where(lax.broadcasted_iota(jnp.int32, (SUB, LANES), 0) == m, RIDGE * n_band, 0.0)
            columns.append(total + ident.astype(f32))
        right = list(held)
        iota = lax.broadcasted_iota(jnp.int32, (SUB, LANES), 0)
        for i in range(SUB):
            inverse = 1.0 / columns[i][i : i + 1, :]
            factor = columns[i]
            for group in (columns, right):
                for c in range(len(group)):
                    lead = jnp.broadcast_to(group[c][i : i + 1, :] * inverse, (SUB, LANES))
                    group[c] = jnp.where(iota == i, lead, group[c] - factor * lead)
        for s in range(n_band):
            band = lax.rem(me + n_band - s, n_band)
            gweights[band] = right[s]
            weights[band] = jnp.broadcast_to(
                jnp.sum(right[s] * held[0], axis=0, keepdims=True), (SUB, LANES)
            )

    x_copies = [{} for _ in range(ITERS)]

    ahead = n_band // 2
    behind = n_band - 1 - ahead

    def slot_of(way, distance):
        if distance > behind:
            return n_band - 1
        return distance + way * behind if distance else 0

    def reach_of(k, way):
        return ahead if way == k % 2 else behind

    def send_x(turn, k, way, distance):
        to = slot_of(way, distance + 1)
        copy = pltpu.make_async_remote_copy(
            src_ref=xall.at[turn, k, slot_of(way, distance)],
            dst_ref=xall.at[turn, k, to],
            send_sem=x_send.at[turn, k, to - 1],
            recv_sem=x_recv.at[turn, k, to - 1],
            device_id={"band": nexts[way]},
            device_id_type=MESH,
        )
        copy.start()
        x_copies[turn][(k, way, distance + 1)] = copy

    def pump(turn, distance, chosen=range(dirs)):
        for k in chosen:
            for way in range(2):
                reach = reach_of(k, way)
                if distance <= reach:
                    x_copies[turn][(k, way, distance)].wait_recv()
                    if distance < reach:
                        send_x(turn, k, way, distance)

    def source(slot):
        if slot <= behind:
            return at(lax.rem(pos + n_band - slot, n_band))
        return at(lax.rem(pos + slot - behind, n_band))

    def end(comp, lane):
        return ends[comp * dirs : (comp + 1) * dirs, lane]

    early, late = range(dirs // 2), range(dirs // 2, dirs)
    d_copies = []

    def send_d(turn, n, src, dst, stage):
        copy = pltpu.make_async_remote_copy(
            src_ref=src,
            dst_ref=dst,
            send_sem=d_send.at[turn, n],
            recv_sem=d_recv.at[turn, n],
            device_id={"dir": flip(stage)},
            device_id_type=MESH,
        )
        copy.start()
        d_copies.append(copy)
        return copy

    first = slice(0, base)
    second = slice(base, 2 * base)

    for turn in range(ITERS):
        for g in range(nrow // SUB):
            for j in range(per):
                value = jones[pl.ds(g * SUB * per + j, SUB, stride=per), :]
                left = value
                for piece in range(PIECES):
                    part = left.astype(jnp.bfloat16)
                    lhs[
                        piece * nrow + g * SUB : piece * nrow + (g + 1) * SUB,
                        j * LANES : (j + 1) * LANES,
                    ] = part
                    left = left - part.astype(f32)
        ends[...] = join(jnp.dot(lhs[...], gather_hot[...], preferred_element_type=f32), nrow)

        def model_body(i, carry):
            j = i // halves
            h = lax.rem(i, halves)
            lane = pl.ds(pl.multiple_of(j * LANES, LANES), LANES)
            lane_q = pl.ds(pl.multiple_of(base + j * LANES, LANES), LANES)
            time = pl.ds(pl.multiple_of(h * SUB, SUB), SUB)
            total = [None] * 4
            for k in range(dirs):
                c = [(coh[k, v, time, lane], coh[k, 4 + v, time, lane]) for v in range(4)]

                def spread(v, where):
                    return tuple(
                        jnp.broadcast_to(
                            ends[(4 * part + v) * dirs + k : (4 * part + v) * dirs + k + 1, where],
                            (SUB, LANES),
                        )
                        for part in range(2)
                    )

                p = [spread(v, lane) for v in range(4)]
                q = [spread(v, lane_q) for v in range(4)]
                for a in range(2):
                    b = [cadd(cmul(p[2 * a], c[d]), cmul(p[2 * a + 1], c[2 + d])) for d in range(2)]
                    for d in range(2):
                        term = cadd(cmul_conj(b[0], q[2 * d]), cmul_conj(b[1], q[2 * d + 1]))
                        v = 2 * a + d
                        total[v] = term if total[v] is None else cadd(total[v], term)
            for v in range(4):
                model[turn, 0, v, time, lane] = total[v][0]
                model[turn, 1, v, time, lane] = total[v][1]
            return carry

        lax.fori_loop(0, blocks * halves, model_body, 0)

        other = 1 - own
        hop = send_d(turn, 0, model.at[turn, other], got_a.at[turn], 0)
        jp = [(end(v, first), end(4 + v, first)) for v in range(4)]
        jq = [(end(v, second), end(4 + v, second)) for v in range(4)]

        def gram_of(j):
            m00 = re_mul(j[0], conj(j[0])) + re_mul(j[2], conj(j[2]))
            m11 = re_mul(j[1], conj(j[1])) + re_mul(j[3], conj(j[3]))
            m01 = cadd(cmul_conj(j[1], j[0]), cmul_conj(j[3], j[2]))
            return m00, m11, m01

        m00, m11, m01 = gram_of(jq)
        p00, p11, p01 = gram_of(jp)
        n1_00 = m00 * gram(0, 0) + m11 * gram(1, 1) + 2.0 * re_mul(m01, gram(0, 1))
        n1_11 = m00 * gram(2, 2) + m11 * gram(3, 3) + 2.0 * re_mul(m01, gram(2, 3))
        n1_01 = cadd(
            cadd(scale(m00, gram(0, 2)), scale(m11, gram(1, 3))),
            cadd(cmul(m01, gram(0, 3)), cmul(conj(m01), gram(1, 2))),
        )
        n2_00 = p00 * gram(0, 0) + p11 * gram(2, 2) + 2.0 * re_mul(p01, gram(2, 0))
        n2_11 = p00 * gram(1, 1) + p11 * gram(3, 3) + 2.0 * re_mul(p01, gram(3, 1))
        n2_01 = cadd(
            cadd(scale(p00, gram(1, 0)), scale(p11, gram(3, 2))),
            cadd(cmul(p01, gram(3, 0)), cmul(conj(p01), gram(1, 2))),
        )
        for n, (left, right) in enumerate(
            ((n1_00, n2_00), (n1_11, n2_11), (n1_01[0], n2_01[0]), (n1_01[1], n2_01[1]))
        ):
            vals_n[n * dirs : (n + 1) * dirs, first] = left
            vals_n[n * dirs : (n + 1) * dirs, second] = right

        if turn > 0:
            pump(turn - 1, 1, early)
        hop.wait_recv()
        sum_a[turn, 0] = model[turn, own] + got_a[turn]
        for stage in range(1, stages):
            hop = send_d(turn, stage, sum_a.at[turn, stage - 1], got_b.at[turn, stage - 1], stage)
            if stage == 1:
                if turn > 0:
                    pump(turn - 1, 1, late)
                split_store(lhs_n, 4 * dirs, vals_n[...])
                found = join(jnp.dot(lhs_n[...], scatter_hot[...], preferred_element_type=f32), 4 * dirs)
                for g in range(4 * dirs // SUB):
                    for j in range(per):
                        seg_n[pl.ds(g * SUB * per + j, SUB, stride=per), :] = found[
                            g * SUB : (g + 1) * SUB, j * LANES : (j + 1) * LANES
                        ]
                if turn == 0:
                    start_consensus()
                    solve_weights()
                else:
                    for s in range(2, (ahead + 2) // 2):
                        pump(turn - 1, s)
            hop.wait_recv()
            target = sum_a.at[turn, stage] if stage + 1 < stages else sum_b.at[turn]
            target[...] = sum_a[turn, stage - 1] + got_b[turn, stage - 1]
        hop = send_d(turn, stages, sum_b.at[turn], got_c.at[turn], 0)
        if turn > 0:
            for s in range(max(2, (ahead + 2) // 2), ahead):
                pump(turn - 1, s, early if s + 1 == ahead else range(dirs))
        res[own] = vis[own] - sum_b[turn]
        hop.wait_recv()
        res[other] = vis[other] - got_c[turn]
        if turn > 0 and ahead - 1 >= max(2, (ahead + 2) // 2):
            pump(turn - 1, ahead - 1, late)

        def cross_body(j, carry):
            lane = pl.ds(pl.multiple_of(j * LANES, LANES), LANES)
            r = [[res[v // 4, v % 4, h * SUB : (h + 1) * SUB, lane] for h in range(halves)] for v in range(8)]
            for k in range(dirs):
                c = [[coh[k, v, h * SUB : (h + 1) * SUB, lane] for h in range(halves)] for v in range(8)]
                for a in range(4):
                    for b in range(4):
                        real = sum(r[a][h] * c[b][h] + r[4 + a][h] * c[4 + b][h] for h in range(halves))
                        imag = sum(r[4 + a][h] * c[b][h] - r[a][h] * c[4 + b][h] for h in range(halves))
                        n = 2 * (4 * a + b)
                        cross[n * dirs + k : n * dirs + k + 1, lane] = jnp.sum(real, axis=0, keepdims=True)
                        cross[(n + 1) * dirs + k : (n + 1) * dirs + k + 1, lane] = jnp.sum(
                            imag, axis=0, keepdims=True
                        )
            return carry

        lax.fori_loop(0, blocks, cross_body, 0)

        def crossed(a, b):
            n = 2 * (4 * a + b)
            return (
                cross[n * dirs : (n + 1) * dirs, :],
                cross[(n + 1) * dirs : (n + 2) * dirs, :],
            )

        def herm(which):
            zero = [vals_n[n * dirs : (n + 1) * dirs, which] for n in range(4)]
            return zero[0], zero[1], (zero[2], zero[3])

        for which, j, other_end in ((first, jq, jp), (second, jp, jq)):
            h00, h11, h01 = herm(which)
            for a in range(2):
                for c in range(2):
                    total = None
                    for b in range(2):
                        for d in range(2):
                            if which is first:
                                term = cmul(j[2 * b + d], crossed(2 * a + b, 2 * c + d))
                            else:
                                term = cmul_conj(j[2 * b + d], crossed(2 * b + a, 2 * d + c))
                            total = term if total is None else cadd(total, term)
                    if c == 0:
                        extra = cadd(scale(h00, other_end[2 * a]), cmul_conj(other_end[2 * a + 1], h01))
                    else:
                        extra = cadd(cmul(other_end[2 * a], h01), scale(h11, other_end[2 * a + 1]))
                    total = cadd(total, extra)
                    for part in range(2):
                        n = 4 * part + 2 * a + c
                        vals[n * dirs : (n + 1) * dirs, which] = total[part]

        split_store(lhs, nrow, vals[...])
        found = join(jnp.dot(lhs[...], scatter_hot[...], preferred_element_type=f32), nrow)
        for g in range(nrow // SUB):
            for j in range(per):
                seg[pl.ds(g * SUB * per + j, SUB, stride=per), :] = found[
                    g * SUB : (g + 1) * SUB, j * LANES : (j + 1) * LANES
                ]

        def join_bands(previous):
            pump(previous, ahead)
            for k in range(dirs):
                for v in range(8):
                    here = pl.ds((v * dirs + k) * per, per)
                    total = None
                    for s in range(n_band):
                        term = weights[source(s)] * xall[previous, k, s, v]
                        total = term if total is None else total + term
                    cons[here, :] = total
                    fresh = dual[here, :] + RHO * (jones[here, :] - total)
                    if previous + 1 < ITERS:
                        dual[here, :] = fresh
                    else:
                        dual_out[halves_of(k, v)] = fresh

        if turn > 0:
            join_bands(turn - 1)

        for k in range(dirs):
            def rows_of(v):
                return pl.ds((v * dirs + k) * per, per)

            y = []
            for v in range(8):
                here = rows_of(v)
                y.append(seg[here, :] + RHO * cons[here, :] - dual[here, :])
            h00, h11, re01, im01 = [seg_n[rows_of(n), :] for n in range(4)]
            h00 = h00 + RHO
            h11 = h11 + RHO
            inverse = 1.0 / (h00 * h11 - (re01 * re01 + im01 * im01))
            h00, h11, h01 = h00 * inverse, h11 * inverse, (re01 * inverse, im01 * inverse)
            for a in range(2):
                y0, y1 = (y[2 * a], y[4 + 2 * a]), (y[2 * a + 1], y[4 + 2 * a + 1])
                minus0, minus1 = cmul_conj(y1, h01), cmul(y0, h01)
                for part in range(2):
                    for c in range(2):
                        if c == 0:
                            value = h11 * y0[part] - minus0[part]
                        else:
                            value = h00 * y1[part] - minus1[part]
                        v = 4 * part + 2 * a + c
                        here = rows_of(v)
                        jones[here, :] = value
                        if turn + 1 == ITERS:
                            jones_out[halves_of(k, v)] = value
                        xall[turn, k, 0, v] = value + dual[here, :] * (1.0 / RHO)
            for way in range(2):
                if reach_of(k, way):
                    send_x(turn, k, way, 0)

    last = ITERS - 1
    for s in range(1, ahead):
        pump(last, s)
    join_bands(last)

    def coeff_body(m, carry):
        for k in range(dirs):
            total = [None] * 8
            for s in range(n_band):
                factor = jnp.broadcast_to(gweights[source(s), pl.ds(m, 1), :], (SUB, LANES))
                for v in range(8):
                    term = factor * xall[last, k, s, v]
                    total[v] = term if total[v] is None else total[v] + term
            for v in range(8):
                coeffs[(m,) + halves_of(k, v)] = total[v]
        return carry

    lax.fori_loop(0, SUB, coeff_body, 0)

    for copies in x_copies:
        for copy in copies.values():
            copy.wait_send()
    for copy in d_copies:
        copy.wait_send()


def local(n_band, n_dir, vis, coh, jones_start, dual_start, consensus_start, freq_basis, pairs):
    f32 = jnp.float32
    dirs, times, base = coh.shape[1], coh.shape[-2], coh.shape[-1]
    stations = jones_start.shape[-1]
    per = stations // LANES
    nrow = 8 * dirs
    terms = freq_basis.shape[1]

    def enter(value):
        lead = value.shape[:-2]
        value = value.reshape(lead + (2, per, LANES))
        return jnp.swapaxes(value, -2, -3).reshape(lead + (2 * per, LANES))

    def leave(value, shape):
        value = value.reshape(value.shape[:-2] + (per, 2, LANES))
        return jnp.swapaxes(value, -2, -3).reshape(shape)

    stages = n_dir.bit_length() - 1
    half = (4, times, base)
    vmem = pl.BlockSpec(memory_space=pltpu.VMEM)
    far = pl.BlockSpec(memory_space=pl.ANY)
    raw = (dirs, 4, 2 * per, LANES)
    raw_out = jax.ShapeDtypeStruct(raw, f32)
    bf16 = jnp.bfloat16
    jones, dual, coeffs = pl.pallas_call(
        functools.partial(kernel, n_band, n_dir, dirs, times, base, stations),
        out_shape=(raw_out, raw_out, jax.ShapeDtypeStruct((terms,) + raw, f32)),
        in_specs=[far, far, vmem, vmem, far, pl.BlockSpec(memory_space=pltpu.SMEM), vmem],
        out_specs=(vmem,) * 3,
        scratch_shapes=[
            pltpu.VMEM((2,) + half, f32),
            pltpu.VMEM((dirs, 8, times, base), f32),
            pltpu.VMEM((terms,) + raw, f32),
            pltpu.VMEM((nrow * per, LANES), f32),
            pltpu.VMEM((nrow * per, LANES), f32),
            pltpu.VMEM((SUB, LANES), f32),
            pltpu.VMEM((2 * base, LANES), jnp.int32),
            pltpu.VMEM((nrow * per, LANES), f32),
            pltpu.VMEM((ITERS, dirs, n_band, 8, per, LANES), f32),
            pltpu.VMEM((n_band, SUB, LANES), f32),
            pltpu.VMEM((n_band, SUB, LANES), f32),
            pltpu.VMEM((n_band, SUB, LANES), f32),
            pltpu.VMEM((stations, 2 * base), bf16),
            pltpu.VMEM((2 * base, stations), bf16),
            pltpu.VMEM((PIECES * nrow, max(stations, 2 * base)), bf16),
            pltpu.VMEM((PIECES * 4 * dirs, 2 * base), bf16),
            pltpu.VMEM((nrow, 2 * base), f32),
            pltpu.VMEM((20 * dirs, base), f32),
            pltpu.VMEM((32 * dirs, base), f32),
            pltpu.VMEM((nrow, 2 * base), f32),
            pltpu.VMEM((4 * dirs, 2 * base), f32),
            pltpu.VMEM((nrow * per, LANES), f32),
            pltpu.VMEM((4 * dirs * per, LANES), f32),
            pltpu.VMEM((ITERS, 2) + half, f32),
            pltpu.VMEM((ITERS,) + half, f32),
            pltpu.VMEM((ITERS, stages - 1) + half, f32),
            pltpu.VMEM((ITERS, stages - 1) + half, f32),
            pltpu.VMEM((ITERS,) + half, f32),
            pltpu.VMEM((ITERS,) + half, f32),
            pltpu.VMEM((2,) + half, f32),
            pltpu.SemaphoreType.DMA((3,)),
            pltpu.SemaphoreType.DMA((n_band,)),
            pltpu.SemaphoreType.DMA((n_band,)),
            pltpu.SemaphoreType.DMA((ITERS, dirs, n_band - 1)),
            pltpu.SemaphoreType.DMA((ITERS, dirs, n_band - 1)),
            pltpu.SemaphoreType.DMA((ITERS, stages + 1)),
            pltpu.SemaphoreType.DMA((ITERS, stages + 1)),
        ],
        compiler_params=pltpu.CompilerParams(
            collective_id=0, has_side_effects=True, vmem_limit_bytes=60 * 1024 * 1024
        ),
    )(
        vis.reshape((2,) + half),
        coh.reshape(dirs, 8, times, base),
        enter(jones_start.reshape((dirs, 4, 2, stations))),
        enter(dual_start.reshape((dirs, 4, 2, stations))),
        enter(consensus_start.reshape((terms, dirs, 4, 2, stations))),
        freq_basis,
        pairs,
    )
    return (
        leave(jones, jones_start.shape),
        leave(dual, jones_start.shape),
        leave(coeffs, consensus_start.shape),
    )


def solution(mesh):
    in_specs = (
        P("band", None, None, None, None, None),
        P("band", "dir", None, None, None, None, None),
        P("band", "dir", None, None, None, None),
        P("band", "dir", None, None, None, None),
        P(None, "dir", None, None, None, None),
        P("band", None),
        P(),
    )
    out_specs = (
        P("band", "dir", None, None, None, None),
        P("band", "dir", None, None, None, None),
        P(None, "dir", None, None, None, None),
    )
    body = functools.partial(local, mesh.shape["band"], mesh.shape["dir"])
    return jax.shard_map(body, mesh=mesh, in_specs=in_specs, out_specs=out_specs, check_vma=False)
```

profile of v0, /device:TPU:0, one launch (start us, length us, event | category | flops | bytes accessed | tf_op | source)
XLA Modules:
  0.0 68.9 jit_solution(2636064341035616390)
XLA Ops:
  0.6 63.7 %shard_map.94 = (f32[4,4,16,128]{3,2,1,0:T(8,128)}, f32[4,4,16,128]{3,2,1,0:T(8,128)}, f32[8,4,4,16,128]{4,3,2,1,0:T(8,128)}) custom-call(f32[2,4,16,512]{3,2,1,0:T(8,128)} %bitcast.35, f32[4,8,16,512]{3,2,1,0:T(8,128)} %bitcast.32, f32[4,4,16,128]{3,2,1,0:T(8,128)} %bitcast.36, f32[4,4,16,128]{3,2,1,0:T(8,128)} %bitcast.37, f32[8,4,4,16,128]{4,3,2,1,0:T(8,128)} %bitcast.33, ...), custom_call_target="tpu_custom_call" | custom-call | tf_op jit(solution)/shard_map/pallas_call | solution.py:570
  64.3 0.0 copy-start
  64.3 1.6 %copy.19 = f32[1,4,2,2,2,1024]{5,4,3,2,1,0:T(2,128)} copy(f32[1,4,2,2,2,1024]{5,4,3,2,1,0:T(2,128)} %bitcast.39) | data formatting | bytes 262144
  66.0 0.0 copy-done
  66.0 0.7 copy.20
  66.6 2.3 %copy.21 = f32[8,4,2,2,2,1024]{5,4,3,2,1,0:T(2,128)} copy(f32[8,4,2,2,2,1024]{5,4,3,2,1,0:T(2,128)} %bitcast.34) | data formatting | bytes 2097152
Async XLA Ops:
  64.3 1.6 %copy-start = (f32[4,4,16,128]{3,2,1,0:T(8,128)S(1)}, f32[4,4,16,128]{3,2,1,0:T(8,128)}, u32[]{:S(2)}) copy-start(f32[4,4,16,128]{3,2,1,0:T(8,128)} %get-tuple-element.7) | copy-start | bytes 393220
where the time goes:
time: 69.1 us; the launch traced here: 68.9 us
  Pallas kernels  63.7 us (92%)
  local copies, waits for them, and re-layouts  4.57 us (7%)
    pallas_call x1, Pallas kernels, local(): pl.pallas_call(functools.partial(kernel, n_band, n_dir, dirs, times, base...  63.7 us
    unnamed x5, local copies, waits for them, and re-layouts  4.57 us

commit v1 on v0

v1 whole, which is shorter than its diff:
```python
import functools

import jax
import jax.numpy as jnp
from jax import lax
from jax.experimental import pallas as pl
from jax.experimental.pallas import tpu as pltpu
from jax.sharding import PartitionSpec as P

ITERS = 3
RHO = 5.0
RIDGE = 0.25
LANES = 128
SUB = 8
PIECES = 3
ANSWER = 1
MESH = pl.DeviceIdType.MESH


def cmul(a, b):
    return (a[0] * b[0] - a[1] * b[1], a[0] * b[1] + a[1] * b[0])


def cmul_conj(a, b):
    return (a[0] * b[0] + a[1] * b[1], a[1] * b[0] - a[0] * b[1])


def cadd(a, b):
    return (a[0] + b[0], a[1] + b[1])


def conj(a):
    return (a[0], -a[1])


def re_mul(a, b):
    return a[0] * b[0] - a[1] * b[1]


def scale(r, a):
    return (r * a[0], r * a[1])


def split_store(ref, rows, value):
    left = value
    for piece in range(PIECES):
        part = left.astype(jnp.bfloat16)
        ref[piece * rows : (piece + 1) * rows, :] = part
        if piece + 1 < PIECES:
            left = left - part.astype(jnp.float32)


def join(value, rows):
    total = value[0:rows]
    for piece in range(1, PIECES):
        total = total + value[piece * rows : (piece + 1) * rows]
    return total


def kernel(
    n_band, n_dir, dirs, times, base, stations,
    vis_far, coh_far, jones0_far, dual0_far, coeffs0_far, basis_far, pairs_far,
    jones_out, dual_out, coeffs,
    vis, coh, jones0, dual0, coeffs0, basis, pairs_ref,
    jones, dual, row, ids_col,
    cons, xall, rows_all, weights, gweights, wmat,
    xs, inbox, outbox, consin,
    gather_hot, scatter_hot, lhs, lhs_c, lhs_n, ends, grams, cross, vals, vals_n, found, seg, seg_n,
    model, got_a, sums, got_b, got_c, res,
    load_sem, row_send, row_recv, p_send, p_recv, x_send, x_recv, d_send, d_recv,
):
    f32 = jnp.float32
    nrow = 8 * dirs
    per = stations // LANES
    me = lax.axis_index("band")
    mine = lax.axis_index("dir")
    chunks = base // LANES
    halves = times // SUB
    stages = n_dir.bit_length() - 1
    part_rows = nrow * per // n_band
    exchange = by_chunks(n_band, nrow * per)

    def at(pos):
        half = pos // (n_band // 2)
        return (1 - half) * (2 * pos) + half * (2 * (n_band - 1 - pos) + 1)

    odd = lax.rem(me, 2)
    pos = (1 - odd) * (me // 2) + odd * (n_band - 1 - me // 2)
    nexts = (at(lax.rem(pos + 1, n_band)), at(lax.rem(pos + n_band - 1, n_band)))

    def flip_bits(index, mask):
        out = index
        for b in range(mask.bit_length()):
            if mask >> b & 1:
                out = out + (1 - 2 * lax.rem(index // (1 << b), 2)) * (1 << b)
        return out

    def to_of(step):
        return flip_bits(me, step) if power_of_two(n_band) else lax.rem(me + step, n_band)

    def from_of(step):
        return flip_bits(me, step) if power_of_two(n_band) else lax.rem(me + n_band - step, n_band)

    def flip(stage):
        return flip_bits(mine, 1 << stage)

    def drain(ref, sem):
        pltpu.make_async_copy(ref, ref, sem).wait()

    own = lax.rem(mine, 2)
    other = 1 - own

    loads = {}
    for n, (name, source_ref, near) in enumerate((
        ("pairs", pairs_far, pairs_ref),
        ("jones", jones0_far, jones0),
        ("coh", coh_far, coh),
        ("basis", basis_far, basis),
        ("vis", vis_far, vis),
        ("dual", dual0_far, dual0),
        ("coeffs", coeffs0_far, coeffs0),
    )):
        loads[name] = pltpu.make_async_copy(source_ref, near, load_sem.at[n])
        loads[name].start()

    barrier = pltpu.get_barrier_semaphore()
    for step in range(1, n_band):
        pl.semaphore_signal(barrier, inc=1, device_id={"band": to_of(step)}, device_id_type=MESH)
    for stage in range(stages):
        pl.semaphore_signal(barrier, inc=1, device_id={"dir": flip(stage)}, device_id_type=MESH)

    def halves_of(k, v):
        return (k, v // 2, pl.ds(v % 2, per, stride=2), slice(None))

    def packed(k, v):
        return pl.ds((v * dirs + k) * per, per)

    def block_of(j):
        return j % 2, (j // 2) * LANES

    step_rows = 32

    def hot_body(i, carry):
        start = pl.multiple_of(i * step_rows, step_rows)
        for j in range(2 * chunks):
            lane = slice(j * LANES, (j + 1) * LANES)
            sid = lax.broadcasted_iota(jnp.int32, (step_rows, LANES), 0) + i * step_rows
            which, low = block_of(j)
            ids = pairs_ref[which : which + 1, low : low + LANES]
            same = sid == jnp.broadcast_to(ids, (step_rows, LANES))
            gather_hot[pl.ds(start, step_rows), lane] = jnp.where(same, 1.0, 0.0).astype(jnp.bfloat16)
        return carry

    loads["pairs"].wait()
    lax.fori_loop(0, stations // step_rows, hot_body, 0)

    loads["jones"].wait()
    for k in range(dirs):
        for v in range(8):
            jones[packed(k, v), :] = jones0[halves_of(k, v)]

    def scatter_setup():
        for j in range(2 * chunks):
            which, low = block_of(j)
            ids = jnp.broadcast_to(pairs_ref[which : which + 1, low : low + LANES], (LANES, LANES))
            ids_col[j * LANES : (j + 1) * LANES, :] = jnp.transpose(ids)

        def hot_body2(i, carry):
            start = pl.multiple_of(i * step_rows, step_rows)
            col = ids_col[pl.ds(start, step_rows), :]
            for j in range(stations // LANES):
                lane = slice(j * LANES, (j + 1) * LANES)
                sid = lax.broadcasted_iota(jnp.int32, (step_rows, LANES), 1) + j * LANES
                scatter_hot[pl.ds(start, step_rows), lane] = jnp.where(sid == col, 1.0, 0.0).astype(jnp.bfloat16)
            return carry

        lax.fori_loop(0, 2 * base // step_rows, hot_body2, 0)

    def first_sends():
        pl.semaphore_wait(barrier, n_band - 1 + stages)
        loads["basis"].wait()
        row[...] = jnp.zeros((SUB, LANES), f32)
        for m in range(SUB):
            row[m : m + 1, :] = jnp.full((1, LANES), basis[0, m], f32)
        for step in range(1, n_band):
            pltpu.make_async_remote_copy(
                src_ref=row,
                dst_ref=rows_all.at[step],
                send_sem=row_send.at[0],
                recv_sem=row_recv.at[0],
                device_id={"band": to_of(step)},
                device_id_type=MESH,
            ).start()

    pairs = [(a, b) for a in range(4) for b in range(a, 4)]

    def gram_body(j, carry):
        lane = pl.ds(pl.multiple_of(j * LANES, LANES), LANES)
        for k in range(dirs):
            c = [
                [coh[k, v, h * SUB : (h + 1) * SUB, lane] for h in range(halves)]
                for v in range(8)
            ]
            for n, (a, b) in enumerate(pairs):
                real = sum(c[a][h] * c[b][h] + c[4 + a][h] * c[4 + b][h] for h in range(halves))
                grams[(2 * n) * dirs + k : (2 * n) * dirs + k + 1, lane] = jnp.sum(real, axis=0, keepdims=True)
                if a != b:
                    imag = sum(c[4 + a][h] * c[b][h] - c[a][h] * c[4 + b][h] for h in range(halves))
                    grams[(2 * n + 1) * dirs + k : (2 * n + 1) * dirs + k + 1, lane] = jnp.sum(
                        imag, axis=0, keepdims=True
                    )
        return carry

    def start_consensus():
        loads["coeffs"].wait()
        loads["dual"].wait()
        for k in range(dirs):
            for v in range(8):
                dual[packed(k, v), :] = dual0[halves_of(k, v)]
                total = basis[0, 0] * coeffs0[(0,) + halves_of(k, v)]
                for m in range(1, SUB):
                    total = total + basis[0, m] * coeffs0[(m,) + halves_of(k, v)]
                cons[packed(k, v), :] = total

    def solve_weights():
        drain(rows_all.at[pl.ds(1, n_band - 1)], row_recv.at[0])
        rows_all[0] = row[...]
        held = [rows_all[s] for s in range(n_band)]
        columns = []
        for m in range(SUB):
            total = held[0] * held[0][m : m + 1, :]
            for s in range(1, n_band):
                total = total + held[s] * held[s][m : m + 1, :]
            ident = jnp.where(lax.broadcasted_iota(jnp.int32, (SUB, LANES), 0) == m, RIDGE * n_band, 0.0)
            columns.append(total + ident.astype(f32))
        right = list(held)
        iota = lax.broadcasted_iota(jnp.int32, (SUB, LANES), 0)
        for i in range(SUB):
            inverse = 1.0 / columns[i][i : i + 1, :]
            factor = columns[i]
            for group in (columns, right):
                for c in range(len(group)):
                    lead = jnp.broadcast_to(group[c][i : i + 1, :] * inverse, (SUB, LANES))
                    group[c] = jnp.where(iota == i, lead, group[c] - factor * lead)

        def weight_of(a, b):
            return jnp.broadcast_to(jnp.sum(right[b] * held[a], axis=0, keepdims=True), (SUB, LANES))

        for s in range(n_band):
            band = from_of(s)
            gweights[band] = right[s]
            weights[band] = weight_of(0, s)
        if exchange:
            for a in range(n_band):
                for b in range(n_band):
                    wmat[a * n_band + b] = weight_of(a, b)

    x_copies = [{} for _ in range(ITERS)]
    ahead = n_band // 2
    behind = n_band - 1 - ahead

    def ring(turn):
        return 0 if exchange else turn

    def slot_of(way, distance):
        if distance > behind:
            return n_band - 1
        return distance + way * behind if distance else 0

    def reach_of(k, way):
        return ahead if way == k % 2 else behind

    def send_x(turn, k, way, distance):
        to = slot_of(way, distance + 1)
        copy = pltpu.make_async_remote_copy(
            src_ref=xall.at[ring(turn), k, slot_of(way, distance)],
            dst_ref=xall.at[ring(turn), k, to],
            send_sem=x_send.at[0],
            recv_sem=x_recv.at[ring(turn), k, to - 1],
            device_id={"band": nexts[way]},
            device_id_type=MESH,
        )
        copy.start()
        x_copies[turn][(k, way, distance + 1)] = copy

    def pump(turn, distance, chosen=range(dirs)):
        for k in chosen:
            for way in range(2):
                reach = reach_of(k, way)
                if distance <= reach:
                    x_copies[turn][(k, way, distance)].wait_recv()
                    if distance < reach:
                        send_x(turn, k, way, distance)

    def source(slot):
        if slot <= behind:
            return at(lax.rem(pos + n_band - slot, n_band))
        return at(lax.rem(pos + slot - behind, n_band))

    def part_of(k, v):
        here = (v * dirs + k) * per
        return here // part_rows, pl.ds(here % part_rows, per)

    def send_parts(turn):
        for step in range(n_band - 1, 0, -1):
            pltpu.make_async_remote_copy(
                src_ref=xs.at[turn, to_of(step)],
                dst_ref=inbox.at[turn, step],
                send_sem=p_send.at[0],
                recv_sem=p_recv.at[turn, 0],
                device_id={"band": to_of(step)},
                device_id_type=MESH,
            ).start()

    def answer_parts(turn):
        drain(inbox.at[turn, pl.ds(1, n_band - 1)], p_recv.at[turn, 0])
        inbox[turn, 0] = xs[turn, me]
        for a in range(n_band - 1, -1, -1):
            for r in range(part_rows // SUB):
                here = slice(r * SUB, (r + 1) * SUB)
                total = wmat[a * n_band] * inbox[turn, 0, here, :]
                for b in range(1, n_band):
                    total = total + wmat[a * n_band + b] * inbox[turn, b, here, :]
                outbox[turn, a, here, :] = total
            if a:
                pltpu.make_async_remote_copy(
                    src_ref=outbox.at[turn, a],
                    dst_ref=consin.at[turn, me],
                    send_sem=p_send.at[1],
                    recv_sem=p_recv.at[turn, 1],
                    device_id={"band": to_of(a)},
                    device_id_type=MESH,
                ).start()

    def send_d(turn, n, c, src, dst, stage):
        copy = pltpu.make_async_remote_copy(
            src_ref=src,
            dst_ref=dst,
            send_sem=d_send.at[n],
            recv_sem=d_recv.at[turn, n, c],
            device_id={"dir": flip(stage)},
            device_id_type=MESH,
        )
        copy.start()
        return copy

    def end(comp, lane):
        return ends[comp * dirs : (comp + 1) * dirs, lane]

    def gram(a, b, lane):
        if a > b:
            return conj(gram(b, a, lane))
        n = pairs.index((a, b))
        real = grams[(2 * n) * dirs : (2 * n + 1) * dirs, lane]
        if a == b:
            return real
        return (real, grams[(2 * n + 1) * dirs : (2 * n + 2) * dirs, lane])

    def first_of(c):
        return slice(2 * c * LANES, (2 * c + 1) * LANES)

    def second_of(c):
        return slice((2 * c + 1) * LANES, (2 * c + 2) * LANES)

    def chunk_of(c):
        return slice(c * LANES, (c + 1) * LANES)

    for turn in range(ITERS):
        for g in range(nrow // SUB):
            for j in range(per):
                left = jones[pl.ds(g * SUB * per + j, SUB, stride=per), :]
                for piece in range(PIECES):
                    part = left.astype(jnp.bfloat16)
                    lhs[
                        piece * nrow + g * SUB : piece * nrow + (g + 1) * SUB,
                        j * LANES : (j + 1) * LANES,
                    ] = part
                    left = left - part.astype(f32)
        ends[...] = join(jnp.dot(lhs[...], gather_hot[...], preferred_element_type=f32), nrow)

        def predict(c):
            lane, lane_p, lane_q = chunk_of(c), first_of(c), second_of(c)

            def model_body(h, carry):
                time = pl.ds(pl.multiple_of(h * SUB, SUB), SUB)
                total = [None] * 4
                for k in range(dirs):
                    co = [(coh[k, v, time, lane], coh[k, 4 + v, time, lane]) for v in range(4)]

                    def spread(v, where):
                        return tuple(
                            jnp.broadcast_to(
                                ends[(4 * part + v) * dirs + k : (4 * part + v) * dirs + k + 1, where],
                                (SUB, LANES),
                            )
                            for part in range(2)
                        )

                    p = [spread(v, lane_p) for v in range(4)]
                    q = [spread(v, lane_q) for v in range(4)]
                    for a in range(2):
                        b = [cadd(cmul(p[2 * a], co[d]), cmul(p[2 * a + 1], co[2 + d])) for d in range(2)]
                        for d in range(2):
                            term = cadd(cmul_conj(b[0], q[2 * d]), cmul_conj(b[1], q[2 * d + 1]))
                            v = 2 * a + d
                            total[v] = term if total[v] is None else cadd(total[v], term)
                for v in range(4):
                    model[turn, c, 0, v, time, :] = total[v][0]
                    model[turn, c, 1, v, time, :] = total[v][1]
                return carry

            lax.fori_loop(0, halves, model_body, 0)

        if turn == 0:
            loads["coh"].wait()
        hops = []
        for c in range(chunks):
            predict(c)
            if turn == 0 and c == 0:
                first_sends()
            hops.append(send_d(turn, 0, c, model.at[turn, c, other], got_a.at[turn, c], 0))

        def step_first(c):
            hops[c].wait_recv()
            sums[turn, 0, c] = model[turn, c, own] + got_a[turn, c]
            n = 1
            if stages > 1:
                hops[c] = send_d(turn, n, c, sums.at[turn, 0, c], got_b.at[turn, 0, c], 1)
            else:
                share(c)

        def share(c):
            hops[c] = send_d(turn, stages, c, sums.at[turn, stages - 1, c], got_c.at[turn, c], 0)
            lane = chunk_of(c)
            res[own, :, :, lane] = vis[own, :, :, lane] - sums[turn, stages - 1, c]

        def step_next(stage, c):
            hops[c].wait_recv()
            sums[turn, stage, c] = sums[turn, stage - 1, c] + got_b[turn, stage - 1, c]
            if stage + 1 < stages:
                hops[c] = send_d(
                    turn, stage + 1, c, sums.at[turn, stage, c], got_b.at[turn, stage, c], stage + 1
                )
            else:
                share(c)

        def gram_of(j):
            m00 = re_mul(j[0], conj(j[0])) + re_mul(j[2], conj(j[2]))
            m11 = re_mul(j[1], conj(j[1])) + re_mul(j[3], conj(j[3]))
            m01 = cadd(cmul_conj(j[1], j[0]), cmul_conj(j[3], j[2]))
            return m00, m11, m01

        def ends_of(lane):
            return [(end(v, lane), end(4 + v, lane)) for v in range(4)]

        def normals(c):
            lane = chunk_of(c)

            def gr(a, b):
                return gram(a, b, lane)

            jp, jq = ends_of(first_of(c)), ends_of(second_of(c))
            m00, m11, m01 = gram_of(jq)
            p00, p11, p01 = gram_of(jp)
            n1_00 = m00 * gr(0, 0) + m11 * gr(1, 1) + 2.0 * re_mul(m01, gr(0, 1))
            n1_11 = m00 * gr(2, 2) + m11 * gr(3, 3) + 2.0 * re_mul(m01, gr(2, 3))
            n1_01 = cadd(
                cadd(scale(m00, gr(0, 2)), scale(m11, gr(1, 3))),
                cadd(cmul(m01, gr(0, 3)), cmul(conj(m01), gr(1, 2))),
            )
            n2_00 = p00 * gr(0, 0) + p11 * gr(2, 2) + 2.0 * re_mul(p01, gr(2, 0))
            n2_11 = p00 * gr(1, 1) + p11 * gr(3, 3) + 2.0 * re_mul(p01, gr(3, 1))
            n2_01 = cadd(
                cadd(scale(p00, gr(1, 0)), scale(p11, gr(3, 2))),
                cadd(cmul(p01, gr(3, 0)), cmul(conj(p01), gr(1, 2))),
            )
            for n, (left, right) in enumerate(
                ((n1_00, n2_00), (n1_11, n2_11), (n1_01[0], n2_01[0]), (n1_01[1], n2_01[1]))
            ):
                vals_n[n * dirs : (n + 1) * dirs, first_of(c)] = left
                vals_n[n * dirs : (n + 1) * dirs, second_of(c)] = right

        def scatter_normals():
            split_store(lhs_n, 4 * dirs, vals_n[...])
            out = join(jnp.dot(lhs_n[...], scatter_hot[...], preferred_element_type=f32), 4 * dirs)
            for g in range(4 * dirs // SUB):
                for j in range(per):
                    seg_n[pl.ds(g * SUB * per + j, SUB, stride=per), :] = out[
                        g * SUB : (g + 1) * SUB, j * LANES : (j + 1) * LANES
                    ]

        def step_last(c):
            hops[c].wait_recv()
            lane = chunk_of(c)
            res[other, :, :, lane] = vis[other, :, :, lane] - got_c[turn, c]
            r = [[res[v // 4, v % 4, h * SUB : (h + 1) * SUB, lane] for h in range(halves)] for v in range(8)]
            for k in range(dirs):
                co = [[coh[k, v, h * SUB : (h + 1) * SUB, lane] for h in range(halves)] for v in range(8)]
                for a in range(4):
                    for b in range(4):
                        real = sum(r[a][h] * co[b][h] + r[4 + a][h] * co[4 + b][h] for h in range(halves))
                        imag = sum(r[4 + a][h] * co[b][h] - r[a][h] * co[4 + b][h] for h in range(halves))
                        n = 2 * (4 * a + b)
                        cross[n * dirs + k : n * dirs + k + 1, lane] = jnp.sum(real, axis=0, keepdims=True)
                        cross[(n + 1) * dirs + k : (n + 1) * dirs + k + 1, lane] = jnp.sum(
                            imag, axis=0, keepdims=True
                        )

            def crossed(a, b):
                n = 2 * (4 * a + b)
                return (
                    cross[n * dirs : (n + 1) * dirs, lane],
                    cross[(n + 1) * dirs : (n + 2) * dirs, lane],
                )

            jp, jq = ends_of(first_of(c)), ends_of(second_of(c))
            for which, j, other_end in ((0, jq, jp), (1, jp, jq)):
                where = second_of(c) if which else first_of(c)
                h00, h11, re01, im01 = [vals_n[n * dirs : (n + 1) * dirs, where] for n in range(4)]
                h01 = (re01, im01)
                for a in range(2):
                    for d in range(2):
                        total = None
                        for b in range(2):
                            for e in range(2):
                                if which == 0:
                                    term = cmul(j[2 * b + e], crossed(2 * a + b, 2 * d + e))
                                else:
                                    term = cmul_conj(j[2 * b + e], crossed(2 * b + a, 2 * e + d))
                                total = term if total is None else cadd(total, term)
                        if d == 0:
                            extra = cadd(scale(h00, other_end[2 * a]), cmul_conj(other_end[2 * a + 1], h01))
                        else:
                            extra = cadd(cmul(other_end[2 * a], h01), scale(h11, other_end[2 * a + 1]))
                        total = cadd(total, extra)
                        for part in range(2):
                            n = 4 * part + 2 * a + d
                            vals[n * dirs : (n + 1) * dirs, which * LANES : (which + 1) * LANES] = total[part]

            split_store(lhs_c, nrow, vals[...])
            rows = slice(2 * c * LANES, (2 * c + 2) * LANES)
            out = join(jnp.dot(lhs_c[...], scatter_hot[rows, :], preferred_element_type=f32), nrow)
            if c > 0:
                out = out + found[...]
            if c + 1 < chunks:
                found[...] = out
            else:
                for g in range(nrow // SUB):
                    for j in range(per):
                        seg[pl.ds(g * SUB * per + j, SUB, stride=per), :] = out[
                            g * SUB : (g + 1) * SUB, j * LANES : (j + 1) * LANES
                        ]

        if turn == 0:
            lax.fori_loop(0, chunks, gram_body, 0)
        for c in range(chunks):
            step_first(c)
        for c in range(chunks):
            normals(c)
        if turn == 0:
            scatter_setup()
        scatter_normals()
        if turn == 0:
            start_consensus()
            solve_weights()
            loads["vis"].wait()
        for stage in range(1, stages):
            for c in range(chunks):
                if stage + 1 == stages and c >= 2:
                    step_last(c - 2)
                step_next(stage, c)
                if turn > 0 and exchange and stage == 1 and c == ANSWER:
                    answer_parts(turn - 1)
        for c in range(max(0, chunks - 2) if stages > 1 else 0, chunks):
            step_last(c)

        def refresh(k, v, total, previous):
            here = packed(k, v)
            fresh = dual[here, :] + RHO * (jones[here, :] - total)
            if previous + 1 < ITERS:
                cons[here, :] = total
                dual[here, :] = fresh
            else:
                dual_out[halves_of(k, v)] = fresh

        def join_parts(previous):
            drain(consin.at[previous, pl.ds(1, n_band - 1)], p_recv.at[previous, 1])
            consin[previous, me] = outbox[previous, 0]
            for k in range(dirs):
                for v in range(8):
                    part, rows = part_of(k, v)
                    refresh(k, v, consin[previous, part, rows, :], previous)

        def ring_sum(turn, k, v, slots, total=None):
            for s in slots:
                term = weights[source(s)] * xall[ring(turn), k, s, v]
                total = term if total is None else total + term
            return total

        if turn > 0:
            if exchange:
                join_parts(turn - 1)
            else:
                for s in range(1, ahead + 1):
                    pump(turn - 1, s)
                for k in range(dirs):
                    for v in range(8):
                        refresh(k, v, ring_sum(turn - 1, k, v, range(n_band)), turn - 1)

        by_ring = turn + 1 == ITERS or not exchange
        for k in range(dirs):
            y = []
            for v in range(8):
                here = packed(k, v)
                y.append(seg[here, :] + RHO * cons[here, :] - dual[here, :])
            h00, h11, re01, im01 = [seg_n[packed(k, n), :] for n in range(4)]
            h00 = h00 + RHO
            h11 = h11 + RHO
            inverse = 1.0 / (h00 * h11 - (re01 * re01 + im01 * im01))
            h00, h11, h01 = h00 * inverse, h11 * inverse, (re01 * inverse, im01 * inverse)
            for a in range(2):
                y0, y1 = (y[2 * a], y[4 + 2 * a]), (y[2 * a + 1], y[4 + 2 * a + 1])
                minus0, minus1 = cmul_conj(y1, h01), cmul(y0, h01)
                for part in range(2):
                    for c in range(2):
                        if c == 0:
                            value = h11 * y0[part] - minus0[part]
                        else:
                            value = h00 * y1[part] - minus1[part]
                        v = 4 * part + 2 * a + c
                        here = packed(k, v)
                        jones[here, :] = value
                        if turn + 1 == ITERS:
                            jones_out[halves_of(k, v)] = value
                        sent = value + dual[here, :] * (1.0 / RHO)
                        if by_ring:
                            xall[ring(turn), k, 0, v] = sent
                        else:
                            chunk, rows = part_of(k, v)
                            xs[turn, chunk, rows, :] = sent
            if by_ring:
                for way in range(2):
                    if reach_of(k, way):
                        send_x(turn, k, way, 0)
        if not by_ring:
            send_parts(turn)

    last = ITERS - 1
    for s in range(1, ahead):
        pump(last, s)

    def coeff_body(slots, first):
        def run(m, carry):
            for k in range(dirs):
                total = [None] * 8 if first else [coeffs[(m,) + halves_of(k, v)] for v in range(8)]
                for s in slots:
                    factor = jnp.broadcast_to(gweights[source(s), pl.ds(m, 1), :], (SUB, LANES))
                    for v in range(8):
                        term = factor * xall[ring(last), k, s, v]
                        total[v] = term if total[v] is None else total[v] + term
                for v in range(8):
                    coeffs[(m,) + halves_of(k, v)] = total[v]
            return carry

        lax.fori_loop(0, SUB, run, 0)

    early = range(n_band - 1)
    coeff_body(early, True)
    for k in range(dirs):
        for v in range(8):
            cons[packed(k, v), :] = ring_sum(last, k, v, early)
    pump(last, ahead)
    late = range(n_band - 1, n_band)
    for k in range(dirs):
        for v in range(8):
            refresh(k, v, ring_sum(last, k, v, late, cons[packed(k, v), :]), last)
    coeff_body(late, False)

    drain(rows_all.at[pl.ds(1, n_band - 1)], row_send.at[0])
    drain(xall.at[:, :, pl.ds(1, n_band - 1)], x_send.at[0])
    if exchange:
        drain(inbox.at[:, pl.ds(1, n_band - 1)], p_send.at[0])
        drain(inbox.at[:, pl.ds(1, n_band - 1)], p_send.at[1])
    drain(got_a, d_send.at[0])
    for stage in range(1, stages):
        drain(got_a, d_send.at[stage])
    drain(got_a, d_send.at[stages])


def flush(*refs):
    count = (len(refs) - 1) // 2
    sem = refs[-1]
    copies = [pltpu.make_async_copy(refs[n], refs[count + n], sem.at[n]) for n in range(count)]
    for copy in copies:
        copy.start()
    for copy in copies:
        copy.wait()


def power_of_two(n):
    return n & (n - 1) == 0


def by_chunks(n_band, rows):
    return power_of_two(n_band) and rows % (n_band * SUB) == 0


def local(n_band, n_dir, vis, coh, jones_start, dual_start, consensus_start, freq_basis, pairs):
    f32 = jnp.float32
    dirs, times, base = coh.shape[1], coh.shape[-2], coh.shape[-1]
    stations = jones_start.shape[-1]
    per = stations // LANES
    nrow = 8 * dirs
    terms = freq_basis.shape[1]

    def enter(value):
        lead = value.shape[:-2]
        value = value.reshape(lead + (2, per, LANES))
        return jnp.swapaxes(value, -2, -3).reshape(lead + (2 * per, LANES))

    def leave(value, shape):
        value = value.reshape(value.shape[:-2] + (per, 2, LANES))
        return jnp.swapaxes(value, -2, -3).reshape(shape)

    stages = n_dir.bit_length() - 1
    chunks = base // LANES
    exchange = by_chunks(n_band, nrow * per)
    rings = 1 if exchange else ITERS
    parts = (ITERS - 1, n_band, max(SUB, nrow * per // n_band), LANES) if exchange else (1, 1, SUB, LANES)
    half = (4, times, base)
    piece = (4, times, LANES)
    vmem = pl.BlockSpec(memory_space=pltpu.VMEM)
    far = pl.BlockSpec(memory_space=pltpu.HBM)
    raw = (dirs, 4, 2 * per, LANES)
    raw_out = jax.ShapeDtypeStruct(raw, f32)
    raw_terms = jax.ShapeDtypeStruct((terms,) + raw, f32)
    bf16 = jnp.bfloat16
    operands = (
        vis.reshape((2,) + half),
        coh.reshape(dirs, 8, times, base),
        enter(jones_start.reshape((dirs, 4, 2, stations))),
        enter(dual_start.reshape((dirs, 4, 2, stations))),
        enter(consensus_start.reshape((terms, dirs, 4, 2, stations))),
        freq_basis,
        pairs,
    )
    results = pl.pallas_call(
        functools.partial(kernel, n_band, n_dir, dirs, times, base, stations),
        out_shape=(pltpu.VMEM(raw, f32), pltpu.VMEM(raw, f32), pltpu.VMEM((terms,) + raw, f32)),
        in_specs=[far] * 7,
        out_specs=(vmem,) * 3,
        scratch_shapes=[
            pltpu.VMEM((2,) + half, f32),
            pltpu.VMEM((dirs, 8, times, base), f32),
            pltpu.VMEM(raw, f32),
            pltpu.VMEM(raw, f32),
            pltpu.VMEM((terms,) + raw, f32),
            pltpu.SMEM(freq_basis.shape, f32),
            pltpu.VMEM((2, base), jnp.int32),
            pltpu.VMEM((nrow * per, LANES), f32),
            pltpu.VMEM((nrow * per, LANES), f32),
            pltpu.VMEM((SUB, LANES), f32),
            pltpu.VMEM((2 * base, LANES), jnp.int32),
            pltpu.VMEM((nrow * per, LANES), f32),
            pltpu.VMEM((rings, dirs, n_band, 8, per, LANES), f32),
            pltpu.VMEM((n_band, SUB, LANES), f32),
            pltpu.VMEM((n_band, SUB, LANES), f32),
            pltpu.VMEM((n_band, SUB, LANES), f32),
            pltpu.VMEM((n_band * n_band if exchange else 1, SUB, LANES), f32),
            pltpu.VMEM(parts, f32),
            pltpu.VMEM(parts, f32),
            pltpu.VMEM(parts, f32),
            pltpu.VMEM(parts, f32),
            pltpu.VMEM((stations, 2 * base), bf16),
            pltpu.VMEM((2 * base, stations), bf16),
            pltpu.VMEM((PIECES * nrow, stations), bf16),
            pltpu.VMEM((PIECES * nrow, 2 * LANES), bf16),
            pltpu.VMEM((PIECES * 4 * dirs, 2 * base), bf16),
            pltpu.VMEM((nrow, 2 * base), f32),
            pltpu.VMEM((20 * dirs, base), f32),
            pltpu.VMEM((32 * dirs, base), f32),
            pltpu.VMEM((nrow, 2 * LANES), f32),
            pltpu.VMEM((4 * dirs, 2 * base), f32),
            pltpu.VMEM((nrow, stations), f32),
            pltpu.VMEM((nrow * per, LANES), f32),
            pltpu.VMEM((4 * dirs * per, LANES), f32),
            pltpu.VMEM((ITERS, chunks, 2) + piece, f32),
            pltpu.VMEM((ITERS, chunks) + piece, f32),
            pltpu.VMEM((ITERS, stages, chunks) + piece, f32),
            pltpu.VMEM((ITERS, max(1, stages - 1), chunks) + piece, f32),
            pltpu.VMEM((ITERS, chunks) + piece, f32),
            pltpu.VMEM((2,) + half, f32),
            pltpu.SemaphoreType.DMA((7,)),
            pltpu.SemaphoreType.DMA((1,)),
            pltpu.SemaphoreType.DMA((1,)),
            pltpu.SemaphoreType.DMA((2,)),
            pltpu.SemaphoreType.DMA((ITERS - 1, 2)),
            pltpu.SemaphoreType.DMA((1,)),
            pltpu.SemaphoreType.DMA((rings, dirs, n_band - 1)),
            pltpu.SemaphoreType.DMA((stages + 1,)),
            pltpu.SemaphoreType.DMA((ITERS, stages + 1, chunks)),
        ],
        compiler_params=pltpu.CompilerParams(
            collective_id=0, has_side_effects=True, vmem_limit_bytes=56 * 1024 * 1024
        ),
    )(*[pltpu.with_memory_space_constraint(x, pltpu.HBM) for x in operands])
    jones, dual, coeffs = pl.pallas_call(
        flush,
        out_shape=(raw_out, raw_out, raw_terms),
        in_specs=[vmem] * 3,
        out_specs=(pl.BlockSpec(memory_space=pltpu.HBM),) * 3,
        scratch_shapes=[pltpu.SemaphoreType.DMA((3,))],
        compiler_params=pltpu.CompilerParams(vmem_limit_bytes=1024 * 1024),
    )(*[pltpu.with_memory_space_constraint(x, pltpu.VMEM) for x in results])
    return (
        leave(jones, jones_start.shape),
        leave(dual, jones_start.shape),
        leave(coeffs, consensus_start.shape),
    )


def solution(mesh):
    in_specs = (
        P("band", None, None, None, None, None),
        P("band", "dir", None, None, None, None, None),
        P("band", "dir", None, None, None, None),
        P("band", "dir", None, None, None, None),
        P(None, "dir", None, None, None, None),
        P("band", None),
        P(),
    )
    out_specs = (
        P("band", "dir", None, None, None, None),
        P("band", "dir", None, None, None, None),
        P(None, "dir", None, None, None, None),
    )
    body = functools.partial(local, mesh.shape["band"], mesh.shape["dir"])
    return jax.shard_map(body, mesh=mesh, in_specs=in_specs, out_specs=out_specs, check_vma=False)
```

time: 69.1 us -> 51.5 us (0.75)
  Pallas kernels: 63.7 us -> 50.6 us
  local copies, waits for them, and re-layouts: 4.57 us -> 0 us
    pallas_call x1, Pallas kernels: 63.7 us -> 49.5 us  [local(): pl.pallas_call(functools.partial(kernel, n_band, n_dir, dirs, times, base...]
    unnamed x5 -> x0, local copies, waits for them, and re-layouts: 4.57 us -> none
    pallas_call x0 -> x1, Pallas kernels: none -> 1.08 us  [local(): pl.pallas_call(flush, out_shape=(raw_out, raw_out, raw_terms), in_specs=[...]
where the time goes in v1:
time: 51.5 us; the launch traced here: 51.3 us
  Pallas kernels  50.6 us (98%)
  between operations  0.64 us (1%)
    pallas_call x1, Pallas kernels, local(): pl.pallas_call(functools.partial(kernel, n_band, n_dir, dirs, times, base...  49.5 us
    pallas_call x1, Pallas kernels, local(): pl.pallas_call(flush, out_shape=(raw_out, raw_out, raw_terms), in_specs=[...  1.08 us

profile of v1, /device:TPU:0, one launch (start us, length us, event | category | flops | bytes accessed | tf_op | source)
XLA Modules:
  0.0 51.3 jit_solution(16566286646322120533)
XLA Ops:
  0.6 49.5 %shard_map.94 = (f32[4,4,16,128]{3,2,1,0:T(8,128)S(1)}, f32[4,4,16,128]{3,2,1,0:T(8,128)S(1)}, f32[8,4,4,16,128]{4,3,2,1,0:T(8,128)S(1)}) custom-call(f32[2,4,16,512]{3,2,1,0:T(8,128)} %bitcast.34, f32[4,8,16,512]{3,2,1,0:T(8,128)} %bitcast.32, f32[4,4,16,128]{3,2,1,0:T(8,128)} %bitcast.35, f32[4,4,16,128]{3,2,1,0:T(8,128)} %bitcast.36, ...), custom_call_target="tpu_custom_call" | custom-call | tf_op jit(solution)/shard_map/pallas_call | solution.py:747
  50.2 1.1 %shard_map.95 = (f32[4,4,16,128]{3,2,1,0:T(8,128)}, f32[4,4,16,128]{3,2,1,0:T(8,128)}, f32[8,4,4,16,128]{4,3,2,1,0:T(8,128)}) custom-call(f32[4,4,16,128]{3,2,1,0:T(8,128)S(1)} %get-tuple-element.9.refs_0_, f32[4,4,16,128]{3,2,1,0:T(8,128)S(1)} %get-tuple-element.10.refs_1_, f32[8,4,4,16,128]{4,3,2,1,0:T(8,128)S(1)} %get-tuple-element.11.refs_2_), custom_call_target="tpu_custom_call" | custom-call | tf_op jit(solution)/shard_map/pallas_call | solution.py:807

commit v2 on v1

--- a/solution.py
+++ b/solution.py
@@ -13,7 +13,7 @@
 LANES = 128
 SUB = 8
 PIECES = 3
-ANSWER = 1
+ANSWER = 0
 MESH = pl.DeviceIdType.MESH
 
 
@@ -267,30 +267,39 @@
             return n_band - 1
         return distance + way * behind if distance else 0
 
-    def reach_of(k, way):
-        return ahead if way == k % 2 else behind
-
-    def send_x(turn, k, way, distance):
+    cuts = ring_cuts(exchange)
+    units = dirs * cuts
+
+    def reach_of(u, way):
+        return ahead if way == u % 2 else behind
+
+    order = [
+        (u, way)
+        for pair in zip(*[sorted(range(units), key=lambda u: -reach_of(u, way)) for way in range(2)])
+        for way, u in enumerate(pair)
+    ]
+
+    def send_x(turn, u, way, distance):
         to = slot_of(way, distance + 1)
+        k, rows = u // cuts, pl.ds(u % cuts * (8 // cuts), 8 // cuts)
         copy = pltpu.make_async_remote_copy(
-            src_ref=xall.at[ring(turn), k, slot_of(way, distance)],
-            dst_ref=xall.at[ring(turn), k, to],
+            src_ref=xall.at[ring(turn), k, slot_of(way, distance), rows],
+            dst_ref=xall.at[ring(turn), k, to, rows],
             send_sem=x_send.at[0],
-            recv_sem=x_recv.at[ring(turn), k, to - 1],
+            recv_sem=x_recv.at[ring(turn), u, to - 1],
             device_id={"band": nexts[way]},
             device_id_type=MESH,
         )
         copy.start()
-        x_copies[turn][(k, way, distance + 1)] = copy
-
-    def pump(turn, distance, chosen=range(dirs)):
-        for k in chosen:
-            for way in range(2):
-                reach = reach_of(k, way)
-                if distance <= reach:
-                    x_copies[turn][(k, way, distance)].wait_recv()
-                    if distance < reach:
-                        send_x(turn, k, way, distance)
+        x_copies[turn][(u, way, distance + 1)] = copy
+
+    def pump(turn, distance):
+        for u, way in order:
+            reach = reach_of(u, way)
+            if distance <= reach:
+                x_copies[turn][(u, way, distance)].wait_recv()
+                if distance < reach:
+                    send_x(turn, u, way, distance)
 
     def source(slot):
         if slot <= behind:
@@ -638,11 +647,11 @@
                         else:
                             chunk, rows = part_of(k, v)
                             xs[turn, chunk, rows, :] = sent
-            if by_ring:
-                for way in range(2):
-                    if reach_of(k, way):
-                        send_x(turn, k, way, 0)
-        if not by_ring:
+        if by_ring:
+            for u, way in order:
+                if reach_of(u, way):
+                    send_x(turn, u, way, 0)
+        else:
             send_parts(turn)
 
     last = ITERS - 1
@@ -699,6 +708,10 @@
 
 def power_of_two(n):
     return n & (n - 1) == 0
+
+
+def ring_cuts(exchange):
+    return 2 if exchange else 1
 
 
 def by_chunks(n_band, rows):
@@ -796,7 +809,7 @@
             pltpu.SemaphoreType.DMA((2,)),
             pltpu.SemaphoreType.DMA((ITERS - 1, 2)),
             pltpu.SemaphoreType.DMA((1,)),
-            pltpu.SemaphoreType.DMA((rings, dirs, n_band - 1)),
+            pltpu.SemaphoreType.DMA((rings, dirs * ring_cuts(exchange), n_band - 1)),
             pltpu.SemaphoreType.DMA((stages + 1,)),
             pltpu.SemaphoreType.DMA((ITERS, stages + 1, chunks)),
         ],

time: 51.5 us -> 48.7 us (0.946)
  Pallas kernels: 50.6 us -> 47.9 us
    pallas_call x1, Pallas kernels: 49.5 us -> 46.8 us  [local(): pl.pallas_call(functools.partial(kernel, n_band, n_dir, dirs, times, base...]
where the time goes in v2:
time: 48.7 us; the launch traced here: 48.5 us
  Pallas kernels  47.9 us (98%)
  between operations  0.64 us (1%)
    pallas_call x1, Pallas kernels, local(): pl.pallas_call(functools.partial(kernel, n_band, n_dir, dirs, times, base...  46.8 us
    pallas_call x1, Pallas kernels, local(): pl.pallas_call(flush, out_shape=(raw_out, raw_out, raw_terms), in_specs=[...  1.08 us

profile of v2, /device:TPU:0, one launch (start us, length us, event | category | flops | bytes accessed | tf_op | source)
XLA Modules:
  0.0 48.5 jit_solution(15934243841494568283)
XLA Ops:
  0.6 46.8 %shard_map.94 = (f32[4,4,16,128]{3,2,1,0:T(8,128)S(1)}, f32[4,4,16,128]{3,2,1,0:T(8,128)S(1)}, f32[8,4,4,16,128]{4,3,2,1,0:T(8,128)S(1)}) custom-call(f32[2,4,16,512]{3,2,1,0:T(8,128)} %bitcast.34, f32[4,8,16,512]{3,2,1,0:T(8,128)} %bitcast.32, f32[4,4,16,128]{3,2,1,0:T(8,128)} %bitcast.35, f32[4,4,16,128]{3,2,1,0:T(8,128)} %bitcast.36, ...), custom_call_target="tpu_custom_call" | custom-call | tf_op jit(solution)/shard_map/pallas_call | solution.py:760
  47.4 1.1 %shard_map.95 = (f32[4,4,16,128]{3,2,1,0:T(8,128)}, f32[4,4,16,128]{3,2,1,0:T(8,128)}, f32[8,4,4,16,128]{4,3,2,1,0:T(8,128)}) custom-call(f32[4,4,16,128]{3,2,1,0:T(8,128)S(1)} %get-tuple-element.9.refs_0_, f32[4,4,16,128]{3,2,1,0:T(8,128)S(1)} %get-tuple-element.10.refs_1_, f32[8,4,4,16,128]{4,3,2,1,0:T(8,128)S(1)} %get-tuple-element.11.refs_2_), custom_call_target="tpu_custom_call" | custom-call | tf_op jit(solution)/shard_map/pallas_call | solution.py:820

commit v3 on v2

--- a/solution.py
+++ b/solution.py
@@ -67,7 +67,7 @@
     xs, inbox, outbox, consin,
     gather_hot, scatter_hot, lhs, lhs_c, lhs_n, ends, grams, cross, vals, vals_n, found, seg, seg_n,
     model, got_a, sums, got_b, got_c, res,
-    load_sem, row_send, row_recv, p_send, p_recv, x_send, x_recv, d_send, d_recv,
+    greet_sem, load_sem, row_send, row_recv, p_send, p_recv, x_send, x_recv, d_send, d_recv,
 ):
     f32 = jnp.float32
     nrow = 8 * dirs
@@ -108,7 +108,7 @@
         pltpu.make_async_copy(ref, ref, sem).wait()
 
     own = lax.rem(mine, 2)
-    other = 1 - own
+    leader = mine + 1 - own
 
     loads = {}
     for n, (name, source_ref, near) in enumerate((
@@ -123,12 +123,27 @@
         loads[name] = pltpu.make_async_copy(source_ref, near, load_sem.at[n])
         loads[name].start()
 
+    ways = min(2, n_band - 1)
+    rounds = n_band // 2 - 1 if exchange else 0
+    band_peers = list(nexts[:ways]) if exchange else [to_of(step) for step in range(1, n_band)]
     barrier = pltpu.get_barrier_semaphore()
-    for step in range(1, n_band):
-        pl.semaphore_signal(barrier, inc=1, device_id={"band": to_of(step)}, device_id_type=MESH)
+    for peer in band_peers:
+        pl.semaphore_signal(barrier, inc=1, device_id={"band": peer}, device_id_type=MESH)
     for stage in range(stages):
         pl.semaphore_signal(barrier, inc=1, device_id={"dir": flip(stage)}, device_id_type=MESH)
 
+    def greet(r):
+        if r < rounds:
+            for way in range(ways):
+                pl.semaphore_signal(
+                    greet_sem.at[r], inc=1, device_id={"band": nexts[way]}, device_id_type=MESH
+                )
+
+    def hear(r):
+        if r < rounds:
+            pl.semaphore_wait(greet_sem.at[r], ways)
+            greet(r + 1)
+
     def halves_of(k, v):
         return (k, v // 2, pl.ds(v % 2, per, stride=2), slice(None))
 
@@ -138,28 +153,34 @@
     def block_of(j):
         return j % 2, (j // 2) * LANES
 
-    step_rows = 32
-
-    def hot_body(i, carry):
-        start = pl.multiple_of(i * step_rows, step_rows)
-        for j in range(2 * chunks):
-            lane = slice(j * LANES, (j + 1) * LANES)
+    def gather_setup(c):
+        step_rows = LANES
+
+        def hot_body(i, carry):
+            start = pl.multiple_of(i * step_rows, step_rows)
             sid = lax.broadcasted_iota(jnp.int32, (step_rows, LANES), 0) + i * step_rows
-            which, low = block_of(j)
-            ids = pairs_ref[which : which + 1, low : low + LANES]
-            same = sid == jnp.broadcast_to(ids, (step_rows, LANES))
-            gather_hot[pl.ds(start, step_rows), lane] = jnp.where(same, 1.0, 0.0).astype(jnp.bfloat16)
-        return carry
+            for j in (2 * c, 2 * c + 1):
+                lane = slice(j * LANES, (j + 1) * LANES)
+                which, low = block_of(j)
+                ids = pairs_ref[which : which + 1, low : low + LANES]
+                same = sid == jnp.broadcast_to(ids, (step_rows, LANES))
+                gather_hot[pl.ds(start, step_rows), lane] = jnp.where(same, 1.0, 0.0).astype(jnp.bfloat16)
+            return carry
+
+        lax.fori_loop(0, stations // step_rows, hot_body, 0)
 
     loads["pairs"].wait()
-    lax.fori_loop(0, stations // step_rows, hot_body, 0)
-
+    group = 2 - chunks % 2
+    for c in range(group):
+        gather_setup(c)
     loads["jones"].wait()
     for k in range(dirs):
         for v in range(8):
             jones[packed(k, v), :] = jones0[halves_of(k, v)]
 
     def scatter_setup():
+        step_rows = 32
+
         for j in range(2 * chunks):
             which, low = block_of(j)
             ids = jnp.broadcast_to(pairs_ref[which : which + 1, low : low + LANES], (LANES, LANES))
@@ -177,11 +198,14 @@
         lax.fori_loop(0, 2 * base // step_rows, hot_body2, 0)
 
     def first_sends():
-        pl.semaphore_wait(barrier, n_band - 1 + stages)
+        pl.semaphore_wait(barrier, len(band_peers) + stages)
+        greet(0)
         loads["basis"].wait()
         row[...] = jnp.zeros((SUB, LANES), f32)
         for m in range(SUB):
             row[m : m + 1, :] = jnp.full((1, LANES), basis[0, m], f32)
+
+    def send_rows():
         for step in range(1, n_band):
             pltpu.make_async_remote_copy(
                 src_ref=row,
@@ -314,44 +338,65 @@
         for step in range(n_band - 1, 0, -1):
             pltpu.make_async_remote_copy(
                 src_ref=xs.at[turn, to_of(step)],
-                dst_ref=inbox.at[turn, step],
+                dst_ref=inbox.at[turn, own, step],
+                send_sem=p_send.at[0],
+                recv_sem=p_recv.at[turn, own],
+                device_id={"band": to_of(step), "dir": leader},
+                device_id_type=MESH,
+            ).start()
+
+        @pl.when(own == 0)
+        def _():
+            pltpu.make_async_remote_copy(
+                src_ref=xs.at[turn, me],
+                dst_ref=inbox.at[turn, 0, 0],
                 send_sem=p_send.at[0],
                 recv_sem=p_recv.at[turn, 0],
-                device_id={"band": to_of(step)},
+                device_id={"dir": flip(0)},
                 device_id_type=MESH,
             ).start()
 
-    def answer_parts(turn):
-        drain(inbox.at[turn, pl.ds(1, n_band - 1)], p_recv.at[turn, 0])
-        inbox[turn, 0] = xs[turn, me]
+        @pl.when(own == 1)
+        def _():
+            inbox[turn, 1, 0] = xs[turn, me]
+
+    def answer_parts(turn, side):
+        if side == 0:
+            drain(inbox.at[turn, 0], p_recv.at[turn, 0])
+        else:
+            drain(inbox.at[turn, 1, pl.ds(1, n_band - 1)], p_recv.at[turn, 1])
         for a in range(n_band - 1, -1, -1):
             for r in range(part_rows // SUB):
                 here = slice(r * SUB, (r + 1) * SUB)
-                total = wmat[a * n_band] * inbox[turn, 0, here, :]
+                total = wmat[a * n_band] * inbox[turn, side, 0, here, :]
                 for b in range(1, n_band):
-                    total = total + wmat[a * n_band + b] * inbox[turn, b, here, :]
-                outbox[turn, a, here, :] = total
-            if a:
+                    total = total + wmat[a * n_band + b] * inbox[turn, side, b, here, :]
+                outbox[turn, side, a, here, :] = total
+            if a or side == 0:
                 pltpu.make_async_remote_copy(
-                    src_ref=outbox.at[turn, a],
+                    src_ref=outbox.at[turn, side, a],
                     dst_ref=consin.at[turn, me],
                     send_sem=p_send.at[1],
-                    recv_sem=p_recv.at[turn, 1],
-                    device_id={"band": to_of(a)},
+                    recv_sem=p_recv.at[turn, 2],
+                    device_id={"band": to_of(a), "dir": flip(0)} if side == 0 else {"band": to_of(a)},
                     device_id_type=MESH,
                 ).start()
 
-    def send_d(turn, n, c, src, dst, stage):
-        copy = pltpu.make_async_remote_copy(
+    def send_d(turn, n, c):
+        if n == 0:
+            src, dst = model.at[turn, c], got_a.at[turn, c]
+        elif n < stages:
+            src, dst = sums.at[turn, n - 1, c], got_b.at[turn, n - 1, c]
+        else:
+            src, dst = sums.at[turn, stages - 1, c], got_c.at[turn, c]
+        return pltpu.make_async_remote_copy(
             src_ref=src,
             dst_ref=dst,
             send_sem=d_send.at[n],
             recv_sem=d_recv.at[turn, n, c],
-            device_id={"dir": flip(stage)},
+            device_id={"dir": flip(n if n < stages else 0)},
             device_id_type=MESH,
         )
-        copy.start()
-        return copy
 
     def end(comp, lane):
         return ends[comp * dirs : (comp + 1) * dirs, lane]
@@ -385,7 +430,10 @@
                         j * LANES : (j + 1) * LANES,
                     ] = part
                     left = left - part.astype(f32)
-        ends[...] = join(jnp.dot(lhs[...], gather_hot[...], preferred_element_type=f32), nrow)
+
+        def gather(c):
+            lane = slice(2 * c * LANES, 2 * (c + group) * LANES)
+            ends[:, lane] = join(jnp.dot(lhs[...], gather_hot[:, lane], preferred_element_type=f32), nrow)
 
         def predict(c):
             lane, lane_p, lane_q = chunk_of(c), first_of(c), second_of(c)
@@ -420,38 +468,48 @@
 
             lax.fori_loop(0, halves, model_body, 0)
 
-        if turn == 0:
-            loads["coh"].wait()
-        hops = []
         for c in range(chunks):
+            if c % group == 0:
+                if turn == 0 and c > 0:
+                    for e in range(group):
+                        gather_setup(c + e)
+                gather(c)
+            if turn == 0 and c == 0:
+                loads["coh"].wait()
             predict(c)
             if turn == 0 and c == 0:
                 first_sends()
-            hops.append(send_d(turn, 0, c, model.at[turn, c, other], got_a.at[turn, c], 0))
-
-        def step_first(c):
-            hops[c].wait_recv()
-            sums[turn, 0, c] = model[turn, c, own] + got_a[turn, c]
-            n = 1
+
+            @pl.when(own == 0)
+            def _():
+                send_d(turn, 0, c).start()
+
+        def collect(c):
+            send_d(turn, 0, c).wait_recv()
+            sums[turn, 0, c] = model[turn, c] + got_a[turn, c]
             if stages > 1:
-                hops[c] = send_d(turn, n, c, sums.at[turn, 0, c], got_b.at[turn, 0, c], 1)
-            else:
-                share(c)
-
-        def share(c):
-            hops[c] = send_d(turn, stages, c, sums.at[turn, stages - 1, c], got_c.at[turn, c], 0)
-            lane = chunk_of(c)
-            res[own, :, :, lane] = vis[own, :, :, lane] - sums[turn, stages - 1, c]
-
-        def step_next(stage, c):
-            hops[c].wait_recv()
+                send_d(turn, 1, c).start()
+
+        def collect_next(stage, c):
+            send_d(turn, stage, c).wait_recv()
             sums[turn, stage, c] = sums[turn, stage - 1, c] + got_b[turn, stage - 1, c]
             if stage + 1 < stages:
-                hops[c] = send_d(
-                    turn, stage + 1, c, sums.at[turn, stage, c], got_b.at[turn, stage, c], stage + 1
-                )
-            else:
-                share(c)
+                send_d(turn, stage + 1, c).start()
+
+        def obtain(c):
+            lane = chunk_of(c)
+
+            @pl.when(own == 1)
+            def _():
+                if stages > 1:
+                    collect_next(stages - 1, c)
+                send_d(turn, stages, c).start()
+                res[:, :, :, lane] = vis[:, :, :, lane] - sums[turn, stages - 1, c]
+
+            @pl.when(own == 0)
+            def _():
+                send_d(turn, stages, c).wait_recv()
+                res[:, :, :, lane] = vis[:, :, :, lane] - got_c[turn, c]
 
         def gram_of(j):
             m00 = re_mul(j[0], conj(j[0])) + re_mul(j[2], conj(j[2]))
@@ -498,10 +556,8 @@
                         g * SUB : (g + 1) * SUB, j * LANES : (j + 1) * LANES
                     ]
 
-        def step_last(c):
-            hops[c].wait_recv()
+        def finish(c):
             lane = chunk_of(c)
-            res[other, :, :, lane] = vis[other, :, :, lane] - got_c[turn, c]
             r = [[res[v // 4, v % 4, h * SUB : (h + 1) * SUB, lane] for h in range(halves)] for v in range(8)]
             for k in range(dirs):
                 co = [[coh[k, v, h * SUB : (h + 1) * SUB, lane] for h in range(halves)] for v in range(8)]
@@ -562,26 +618,62 @@
 
         if turn == 0:
             lax.fori_loop(0, chunks, gram_body, 0)
+        if turn > 0:
+            for c in range(chunks):
+                normals(c)
+            scatter_normals()
+
+        @pl.when(own == 1)
+        def _():
+            for c in range(chunks):
+                collect(c)
+
+        if turn == 0:
+            for c in range(chunks):
+                normals(c)
+            hear(0)
+            scatter_setup()
+            scatter_normals()
+            start_consensus()
+            hear(1)
+            loads["vis"].wait()
+        if turn > 0 and exchange:
+
+            @pl.when(own == 1)
+            def _():
+                if turn == 1:
+                    solve_weights()
+                answer_parts(turn - 1, 1)
+
+            if turn == 2:
+
+                @pl.when(own == 0)
+                def _():
+                    solve_weights()
+
+        if turn == 1 and not exchange:
+            solve_weights()
+        if stages > 2:
+
+            @pl.when(own == 1)
+            def _():
+                for stage in range(1, stages - 1):
+                    for c in range(chunks):
+                        collect_next(stage, c)
+
         for c in range(chunks):
-            step_first(c)
-        for c in range(chunks):
-            normals(c)
-        if turn == 0:
-            scatter_setup()
-        scatter_normals()
-        if turn == 0:
-            start_consensus()
-            solve_weights()
-            loads["vis"].wait()
-        for stage in range(1, stages):
-            for c in range(chunks):
-                if stage + 1 == stages and c >= 2:
-                    step_last(c - 2)
-                step_next(stage, c)
-                if turn > 0 and exchange and stage == 1 and c == ANSWER:
-                    answer_parts(turn - 1)
-        for c in range(max(0, chunks - 2) if stages > 1 else 0, chunks):
-            step_last(c)
+            obtain(c)
+            if turn > 0 and exchange and c == ANSWER:
+
+                @pl.when(own == 1)
+                def _():
+                    answer_parts(turn - 1, 0)
+
+            finish(c)
+            if turn == 0 and c == min(1, chunks - 1):
+                for r in range(2, max(2, rounds)):
+                    hear(r)
+                send_rows()
 
         def refresh(k, v, total, previous):
             here = packed(k, v)
@@ -593,8 +685,15 @@
                 dual_out[halves_of(k, v)] = fresh
 
         def join_parts(previous):
-            drain(consin.at[previous, pl.ds(1, n_band - 1)], p_recv.at[previous, 1])
-            consin[previous, me] = outbox[previous, 0]
+            @pl.when(own == 0)
+            def _():
+                drain(consin.at[previous], p_recv.at[previous, 2])
+
+            @pl.when(own == 1)
+            def _():
+                drain(consin.at[previous, pl.ds(1, n_band - 1)], p_recv.at[previous, 2])
+                consin[previous, me] = outbox[previous, 1, 0]
+
             for k in range(dirs):
                 for v in range(8):
                     part, rows = part_of(k, v)
@@ -687,13 +786,21 @@
 
     drain(rows_all.at[pl.ds(1, n_band - 1)], row_send.at[0])
     drain(xall.at[:, :, pl.ds(1, n_band - 1)], x_send.at[0])
-    if exchange:
-        drain(inbox.at[:, pl.ds(1, n_band - 1)], p_send.at[0])
-        drain(inbox.at[:, pl.ds(1, n_band - 1)], p_send.at[1])
-    drain(got_a, d_send.at[0])
-    for stage in range(1, stages):
-        drain(got_a, d_send.at[stage])
-    drain(got_a, d_send.at[stages])
+
+    @pl.when(own == 0)
+    def _():
+        drain(model, d_send.at[0])
+        if exchange:
+            drain(xs, p_send.at[0])
+
+    @pl.when(own == 1)
+    def _():
+        for n in range(1, stages + 1):
+            drain(model, d_send.at[n])
+        if exchange:
+            drain(inbox.at[:, 1, pl.ds(1, n_band - 1)], p_send.at[0])
+            drain(inbox.at[:, 0], p_send.at[1])
+            drain(inbox.at[:, 1, pl.ds(1, n_band - 1)], p_send.at[1])
 
 
 def flush(*refs):
@@ -741,7 +848,7 @@
     rings = 1 if exchange else ITERS
     parts = (ITERS - 1, n_band, max(SUB, nrow * per // n_band), LANES) if exchange else (1, 1, SUB, LANES)
     half = (4, times, base)
-    piece = (4, times, LANES)
+    piece = (2, 4, times, LANES)
     vmem = pl.BlockSpec(memory_space=pltpu.VMEM)
     far = pl.BlockSpec(memory_space=pltpu.HBM)
     raw = (dirs, 4, 2 * per, LANES)
@@ -781,8 +888,8 @@
             pltpu.VMEM((n_band, SUB, LANES), f32),
             pltpu.VMEM((n_band * n_band if exchange else 1, SUB, LANES), f32),
             pltpu.VMEM(parts, f32),
-            pltpu.VMEM(parts, f32),
-            pltpu.VMEM(parts, f32),
+            pltpu.VMEM(parts[:1] + (2,) + parts[1:], f32),
+            pltpu.VMEM(parts[:1] + (2,) + parts[1:], f32),
             pltpu.VMEM(parts, f32),
             pltpu.VMEM((stations, 2 * base), bf16),
             pltpu.VMEM((2 * base, stations), bf16),
@@ -797,17 +904,18 @@
             pltpu.VMEM((nrow, stations), f32),
             pltpu.VMEM((nrow * per, LANES), f32),
             pltpu.VMEM((4 * dirs * per, LANES), f32),
-            pltpu.VMEM((ITERS, chunks, 2) + piece, f32),
+            pltpu.VMEM((ITERS, chunks) + piece, f32),
             pltpu.VMEM((ITERS, chunks) + piece, f32),
             pltpu.VMEM((ITERS, stages, chunks) + piece, f32),
             pltpu.VMEM((ITERS, max(1, stages - 1), chunks) + piece, f32),
             pltpu.VMEM((ITERS, chunks) + piece, f32),
             pltpu.VMEM((2,) + half, f32),
+            pltpu.SemaphoreType.REGULAR((max(1, n_band // 2 - 1) if exchange else 1,)),
             pltpu.SemaphoreType.DMA((7,)),
             pltpu.SemaphoreType.DMA((1,)),
             pltpu.SemaphoreType.DMA((1,)),
             pltpu.SemaphoreType.DMA((2,)),
-            pltpu.SemaphoreType.DMA((ITERS - 1, 2)),
+            pltpu.SemaphoreType.DMA((ITERS - 1, 3)),
             pltpu.SemaphoreType.DMA((1,)),
             pltpu.SemaphoreType.DMA((rings, dirs * ring_cuts(exchange), n_band - 1)),
             pltpu.SemaphoreType.DMA((stages + 1,)),

time: 48.7 us -> 44.5 us (0.914)
  Pallas kernels: 47.9 us -> 43.7 us
    pallas_call x1, Pallas kernels: 46.8 us -> 42.6 us  [local(): pl.pallas_call(functools.partial(kernel, n_band, n_dir, dirs, times, base...]
where the time goes in v3:
time: 44.5 us; the launch traced here: 44.3 us
  Pallas kernels  43.7 us (98%)
  between operations  0.64 us (1%)
    pallas_call x1, Pallas kernels, local(): pl.pallas_call(functools.partial(kernel, n_band, n_dir, dirs, times, base...  42.6 us
    pallas_call x1, Pallas kernels, local(): pl.pallas_call(flush, out_shape=(raw_out, raw_out, raw_terms), in_specs=[...  1.08 us

profile of v3, /device:TPU:0, one launch (start us, length us, event | category | flops | bytes accessed | tf_op | source)
XLA Modules:
  0.0 44.3 jit_solution(11868408618955762978)
XLA Ops:
  0.6 42.6 %shard_map.94 = (f32[4,4,16,128]{3,2,1,0:T(8,128)S(1)}, f32[4,4,16,128]{3,2,1,0:T(8,128)S(1)}, f32[8,4,4,16,128]{4,3,2,1,0:T(8,128)S(1)}) custom-call(f32[2,4,16,512]{3,2,1,0:T(8,128)} %bitcast.34, f32[4,8,16,512]{3,2,1,0:T(8,128)} %bitcast.32, f32[4,4,16,128]{3,2,1,0:T(8,128)} %bitcast.35, f32[4,4,16,128]{3,2,1,0:T(8,128)} %bitcast.36, ...), custom_call_target="tpu_custom_call" | custom-call | tf_op jit(solution)/shard_map/pallas_call | solution.py:867
  43.2 1.1 %shard_map.95 = (f32[4,4,16,128]{3,2,1,0:T(8,128)}, f32[4,4,16,128]{3,2,1,0:T(8,128)}, f32[8,4,4,16,128]{4,3,2,1,0:T(8,128)}) custom-call(f32[4,4,16,128]{3,2,1,0:T(8,128)S(1)} %get-tuple-element.9.refs_0_, f32[4,4,16,128]{3,2,1,0:T(8,128)S(1)} %get-tuple-element.10.refs_1_, f32[8,4,4,16,128]{4,3,2,1,0:T(8,128)S(1)} %get-tuple-element.11.refs_2_), custom_call_target="tpu_custom_call" | custom-call | tf_op jit(solution)/shard_map/pallas_call | solution.py:928

commit v4 on v3

--- a/solution.py
+++ b/solution.py
@@ -67,7 +67,7 @@
     xs, inbox, outbox, consin,
     gather_hot, scatter_hot, lhs, lhs_c, lhs_n, ends, grams, cross, vals, vals_n, found, seg, seg_n,
     model, got_a, sums, got_b, got_c, res,
-    greet_sem, load_sem, row_send, row_recv, p_send, p_recv, x_send, x_recv, d_send, d_recv,
+    greet_sem, load_sem, row_send, row_recv, p_send, p_recv, x_send, x_recv, x_far, d_send, d_recv,
 ):
     f32 = jnp.float32
     nrow = 8 * dirs
@@ -171,8 +171,7 @@
 
     loads["pairs"].wait()
     group = 2 - chunks % 2
-    for c in range(group):
-        gather_setup(c)
+    gather_setup(0)
     loads["jones"].wait()
     for k in range(dirs):
         for v in range(8):
@@ -303,6 +302,22 @@
         for way, u in enumerate(pair)
     ]
 
+    def arrival(turn, u, way, distance):
+        far = reach_of(u, way) == ahead
+        if cuts == 1:
+            return x_recv.at[ring(turn), u, slot_of(way, distance) - 1]
+        if distance == reach_of(u, way):
+            return x_far.at[2 * far + way]
+        return x_recv.at[ring(turn), u, distance - 1 + (0 if far else ahead - 1)]
+
+    def settle(turn, way, distance):
+        half = way if distance == ahead else 1 - way
+        rows = pl.ds(half * (8 // cuts), 8 // cuts)
+        drain(
+            xall.at[ring(turn), :, slot_of(way, distance), rows],
+            x_far.at[2 * (distance == ahead) + way],
+        )
+
     def send_x(turn, u, way, distance):
         to = slot_of(way, distance + 1)
         k, rows = u // cuts, pl.ds(u % cuts * (8 // cuts), 8 // cuts)
@@ -310,7 +325,7 @@
             src_ref=xall.at[ring(turn), k, slot_of(way, distance), rows],
             dst_ref=xall.at[ring(turn), k, to, rows],
             send_sem=x_send.at[0],
-            recv_sem=x_recv.at[ring(turn), u, to - 1],
+            recv_sem=arrival(turn, u, way, distance + 1),
             device_id={"band": nexts[way]},
             device_id_type=MESH,
         )
@@ -320,10 +335,14 @@
     def pump(turn, distance):
         for u, way in order:
             reach = reach_of(u, way)
-            if distance <= reach:
+            if distance < reach:
                 x_copies[turn][(u, way, distance)].wait_recv()
-                if distance < reach:
-                    send_x(turn, u, way, distance)
+                send_x(turn, u, way, distance)
+            elif distance == reach and cuts == 1:
+                x_copies[turn][(u, way, distance)].wait_recv()
+        if cuts == 2 and distance in (behind, ahead):
+            for way in range(2):
+                settle(turn, way, distance)
 
     def source(slot):
         if slot <= behind:
@@ -393,7 +412,7 @@
             src_ref=src,
             dst_ref=dst,
             send_sem=d_send.at[n],
-            recv_sem=d_recv.at[turn, n, c],
+            recv_sem=d_recv.at[0 if n % stages == 0 else 2 * n - 1 + turn % 2, c],
             device_id={"dir": flip(n if n < stages else 0)},
             device_id_type=MESH,
         )
@@ -431,7 +450,7 @@
                     ] = part
                     left = left - part.astype(f32)
 
-        def gather(c):
+        def gather(c, group):
             lane = slice(2 * c * LANES, 2 * (c + group) * LANES)
             ends[:, lane] = join(jnp.dot(lhs[...], gather_hot[:, lane], preferred_element_type=f32), nrow)
 
@@ -468,27 +487,37 @@
 
             lax.fori_loop(0, halves, model_body, 0)
 
-        for c in range(chunks):
-            if c % group == 0:
-                if turn == 0 and c > 0:
-                    for e in range(group):
-                        gather_setup(c + e)
-                gather(c)
-            if turn == 0 and c == 0:
-                loads["coh"].wait()
-            predict(c)
-            if turn == 0 and c == 0:
-                first_sends()
-
-            @pl.when(own == 0)
-            def _():
-                send_d(turn, 0, c).start()
-
         def collect(c):
             send_d(turn, 0, c).wait_recv()
             sums[turn, 0, c] = model[turn, c] + got_a[turn, c]
             if stages > 1:
                 send_d(turn, 1, c).start()
+
+        def collect_all(some):
+            @pl.when(own == 1)
+            def _():
+                for c in some:
+                    collect(c)
+
+        begun = min(1, chunks - 1) if turn == 0 and chunks > 2 else 0
+        for c in range(chunks):
+            width = 1 if turn == 0 and c < group else group
+            if c % width == 0:
+                if turn == 0 and c > 0:
+                    for e in range(width):
+                        gather_setup(c + e)
+                gather(c, width)
+            if turn == 0 and c == 0:
+                loads["coh"].wait()
+            if begun and c == 2:
+                collect_all(range(begun))
+            predict(c)
+            if turn == 0 and c == 0:
+                first_sends()
+
+            @pl.when(own == 0)
+            def _():
+                send_d(turn, 0, c).start()
 
         def collect_next(stage, c):
             send_d(turn, stage, c).wait_recv()
@@ -617,23 +646,17 @@
                         ]
 
         if turn == 0:
+            collect_all(range(begun, begun + 1))
             lax.fori_loop(0, chunks, gram_body, 0)
-        if turn > 0:
-            for c in range(chunks):
-                normals(c)
+        for c in range(chunks):
+            normals(c)
+        if turn == 0:
+            hear(0)
+        else:
             scatter_normals()
-
-        @pl.when(own == 1)
-        def _():
-            for c in range(chunks):
-                collect(c)
-
+        collect_all(range(begun + 1 if turn == 0 else 0, chunks))
         if turn == 0:
-            for c in range(chunks):
-                normals(c)
-            hear(0)
             scatter_setup()
-            scatter_normals()
             start_consensus()
             hear(1)
             loads["vis"].wait()
@@ -669,6 +692,8 @@
                 def _():
                     answer_parts(turn - 1, 0)
 
+            if turn == 0 and c == min(1, chunks - 1):
+                scatter_normals()
             finish(c)
             if turn == 0 and c == min(1, chunks - 1):
                 for r in range(2, max(2, rounds)):
@@ -917,9 +942,10 @@
             pltpu.SemaphoreType.DMA((2,)),
             pltpu.SemaphoreType.DMA((ITERS - 1, 3)),
             pltpu.SemaphoreType.DMA((1,)),
-            pltpu.SemaphoreType.DMA((rings, dirs * ring_cuts(exchange), n_band - 1)),
+            pltpu.SemaphoreType.DMA((rings, dirs * ring_cuts(exchange), max(1, n_band - 3) if exchange else n_band - 1)),
+            pltpu.SemaphoreType.DMA((4,)),
             pltpu.SemaphoreType.DMA((stages + 1,)),
-            pltpu.SemaphoreType.DMA((ITERS, stages + 1, chunks)),
+            pltpu.SemaphoreType.DMA((2 * stages - 1, chunks)),
         ],
         compiler_params=pltpu.CompilerParams(
             collective_id=0, has_side_effects=True, vmem_limit_bytes=56 * 1024 * 1024

time: 44.5 us -> 44 us (0.989)
  Pallas kernels: 43.7 us -> 43.2 us
    pallas_call x1, Pallas kernels: 42.6 us -> 42.1 us  [local(): pl.pallas_call(functools.partial(kernel, n_band, n_dir, dirs, times, base...]
where the time goes in v4:
time: 44 us; the launch traced here: 43.9 us
  Pallas kernels  43.2 us (98%)
  between operations  0.64 us (1%)
    pallas_call x1, Pallas kernels, local(): pl.pallas_call(functools.partial(kernel, n_band, n_dir, dirs, times, base...  42.1 us
    pallas_call x1, Pallas kernels, local(): pl.pallas_call(flush, out_shape=(raw_out, raw_out, raw_terms), in_specs=[...  1.08 us

profile of v4, /device:TPU:0, one launch (start us, length us, event | category | flops | bytes accessed | tf_op | source)
XLA Modules:
  0.0 43.9 jit_solution(8443812304018889267)
XLA Ops:
  0.6 42.1 %shard_map.94 = (f32[4,4,16,128]{3,2,1,0:T(8,128)S(1)}, f32[4,4,16,128]{3,2,1,0:T(8,128)S(1)}, f32[8,4,4,16,128]{4,3,2,1,0:T(8,128)S(1)}) custom-call(f32[2,4,16,512]{3,2,1,0:T(8,128)} %bitcast.34, f32[4,8,16,512]{3,2,1,0:T(8,128)} %bitcast.32, f32[4,4,16,128]{3,2,1,0:T(8,128)} %bitcast.35, f32[4,4,16,128]{3,2,1,0:T(8,128)} %bitcast.36, ...), custom_call_target="tpu_custom_call" | custom-call | tf_op jit(solution)/shard_map/pallas_call | solution.py:892
  42.8 1.1 %shard_map.95 = (f32[4,4,16,128]{3,2,1,0:T(8,128)}, f32[4,4,16,128]{3,2,1,0:T(8,128)}, f32[8,4,4,16,128]{4,3,2,1,0:T(8,128)}) custom-call(f32[4,4,16,128]{3,2,1,0:T(8,128)S(1)} %get-tuple-element.9.refs_0_, f32[4,4,16,128]{3,2,1,0:T(8,128)S(1)} %get-tuple-element.10.refs_1_, f32[8,4,4,16,128]{4,3,2,1,0:T(8,128)S(1)} %get-tuple-element.11.refs_2_), custom_call_target="tpu_custom_call" | custom-call | tf_op jit(solution)/shard_map/pallas_call | solution.py:954

commit v5 on v4

--- a/solution.py
+++ b/solution.py
@@ -110,18 +110,25 @@
     own = lax.rem(mine, 2)
     leader = mine + 1 - own
 
-    loads = {}
-    for n, (name, source_ref, near) in enumerate((
-        ("pairs", pairs_far, pairs_ref),
-        ("jones", jones0_far, jones0),
-        ("coh", coh_far, coh),
+    def columns_of(c):
+        return (slice(None), slice(None), slice(None), pl.ds(c * LANES, LANES))
+
+    cuts_of = [(c, coh_far.at[columns_of(c)], coh.at[columns_of(c)]) for c in range(chunks)]
+    urgent = [("pairs", pairs_far, pairs_ref), ("jones", jones0_far, jones0), cuts_of[0]]
+    patient = cuts_of[1:] + [
         ("basis", basis_far, basis),
         ("vis", vis_far, vis),
         ("dual", dual0_far, dual0),
         ("coeffs", coeffs0_far, coeffs0),
-    )):
-        loads[name] = pltpu.make_async_copy(source_ref, near, load_sem.at[n])
-        loads[name].start()
+    ]
+    loads = {}
+
+    def load(some):
+        for name, source_ref, near in some:
+            loads[name] = pltpu.make_async_copy(source_ref, near, load_sem.at[len(loads)])
+            loads[name].start()
+
+    load(urgent)
 
     ways = min(2, n_band - 1)
     rounds = n_band // 2 - 1 if exchange else 0
@@ -170,6 +177,7 @@
         lax.fori_loop(0, stations // step_rows, hot_body, 0)
 
     loads["pairs"].wait()
+    load(patient)
     group = 2 - chunks % 2
     gather_setup(0)
     loads["jones"].wait()
@@ -507,8 +515,8 @@
                     for e in range(width):
                         gather_setup(c + e)
                 gather(c, width)
-            if turn == 0 and c == 0:
-                loads["coh"].wait()
+            if turn == 0:
+                loads[c].wait()
             if begun and c == 2:
                 collect_all(range(begun))
             predict(c)
@@ -936,7 +944,7 @@
             pltpu.VMEM((ITERS, chunks) + piece, f32),
             pltpu.VMEM((2,) + half, f32),
             pltpu.SemaphoreType.REGULAR((max(1, n_band // 2 - 1) if exchange else 1,)),
-            pltpu.SemaphoreType.DMA((7,)),
+            pltpu.SemaphoreType.DMA((6 + chunks,)),
             pltpu.SemaphoreType.DMA((1,)),
             pltpu.SemaphoreType.DMA((1,)),
             pltpu.SemaphoreType.DMA((2,)),

time: 44 us -> 44.1 us (level)
  no operation moved by 1% of the time
where the time goes in v5:
time: 44.1 us; the launch traced here: 43.9 us
  Pallas kernels  43.2 us (98%)
  between operations  0.64 us (1%)
    pallas_call x1, Pallas kernels, local(): pl.pallas_call(functools.partial(kernel, n_band, n_dir, dirs, times, base...  42.2 us
    pallas_call x1, Pallas kernels, local(): pl.pallas_call(flush, out_shape=(raw_out, raw_out, raw_terms), in_specs=[...  1.08 us

profile of v5, /device:TPU:0, one launch (start us, length us, event | category | flops | bytes accessed | tf_op | source)
XLA Modules:
  0.0 43.9 jit_solution(14188899267574130821)
XLA Ops:
  0.6 42.2 %shard_map.94 = (f32[4,4,16,128]{3,2,1,0:T(8,128)S(1)}, f32[4,4,16,128]{3,2,1,0:T(8,128)S(1)}, f32[8,4,4,16,128]{4,3,2,1,0:T(8,128)S(1)}) custom-call(f32[2,4,16,512]{3,2,1,0:T(8,128)} %bitcast.34, f32[4,8,16,512]{3,2,1,0:T(8,128)} %bitcast.32, f32[4,4,16,128]{3,2,1,0:T(8,128)} %bitcast.35, f32[4,4,16,128]{3,2,1,0:T(8,128)} %bitcast.36, ...), custom_call_target="tpu_custom_call" | custom-call | tf_op jit(solution)/shard_map/pallas_call | solution.py:900
  42.8 1.1 %shard_map.95 = (f32[4,4,16,128]{3,2,1,0:T(8,128)}, f32[4,4,16,128]{3,2,1,0:T(8,128)}, f32[8,4,4,16,128]{4,3,2,1,0:T(8,128)}) custom-call(f32[4,4,16,128]{3,2,1,0:T(8,128)S(1)} %get-tuple-element.9.refs_0_, f32[4,4,16,128]{3,2,1,0:T(8,128)S(1)} %get-tuple-element.10.refs_1_, f32[8,4,4,16,128]{4,3,2,1,0:T(8,128)S(1)} %get-tuple-element.11.refs_2_), custom_call_target="tpu_custom_call" | custom-call | tf_op jit(solution)/shard_map/pallas_call | solution.py:962
